TPU v7x, 32 devices: a whole 2x2x4 slice. The times are simulated.
32 devices in a mesh: groups: 2 (over y), rows: 4 (over z), cols: 4 (over x, core).
Axes of the slice: x: 2, y: 2, z: 4, core: 2. Of those that a mesh axis runs over, the one named last changes fastest.
Arguments:
- latent: bfloat16 [4, 32, 16], P(None, ('groups', 'rows'), 'cols'), parts along dimension 1, may hold values from -6 to 6
- w_in: bfloat16 [9, 4, 512], replicated, may hold values from -1 to 1
- w_mid: bfloat16 [9, 256, 512], replicated, may hold values from -0.09375 to 0.09375
- w_low: bfloat16 [9, 128, 256], replicated, may hold values from -0.125 to 0.125
- w_out: bfloat16 [9, 3, 128], replicated, may hold values from -0.1875 to 0.1875
- ramp_rows: int32 [4, 32], replicated, may hold values from 0 to 8, as said below
- ramp_cols: int32 [4, 32], replicated, may hold values from 0 to 8, as said below
- intersection_rows: int32 [4], replicated, may hold values from 1 to 8
- intersection_cols: int32 [4], replicated, may hold values from 1 to 8
Outputs:
- image: float32 [3, 128, 64], P(None, ('groups', 'rows'), 'cols'), parts along dimension 1
There are 2 independent parts, one for each index of `groups`. A program takes and returns all parts, laid end to end along the dimension named above; an argument that names none is the same for every part. Nothing has to cross between parts.
Inputs may be any that keep to these rules, and one draw needn't show every extreme that they name: `ramp_rows`: entries at the inner 4 * 4 pixels of each row of the table are 1 or more. `ramp_cols`: entries at the inner 4 * 4 pixels of each row of the table are 1 or more.
All inputs are finite; a program needn't handle non-finite values.
Results may differ from a plain program's by a relative error of at most 0.0049.
Values may be sent and summed in bfloat16 or wider, within the bound.
A program may use at most 64 MiB of HBM per device.

v0:
```python
import functools

import jax
import jax.numpy as jnp
from jax import lax
from jax.experimental import pallas as pl
from jax.experimental.pallas import tpu as pltpu
from jax.sharding import PartitionSpec as P

MESH = pl.DeviceIdType.MESH
NGROUPS = 32
HALO = 2
F32 = jnp.float32
BF16 = jnp.bfloat16
AROUND = [(dr, dc) for dr in (-1, 0, 1) for dc in (-1, 0, 1) if (dr, dc) != (0, 0)]
FAR_FIRST = sorted(enumerate(AROUND), key=lambda e: -abs(e[1][0]) - abs(e[1][1]))


def iota(shape, dim):
    return lax.broadcasted_iota(jnp.int32, shape, dim)


def nt_dot(a, b):
    return lax.dot_general(a, b, (((1,), (1,)), ((), ())), preferred_element_type=F32)


def dot(a, b):
    return jnp.dot(a, b, preferred_element_type=F32)


def down(x):
    return jnp.concatenate([jnp.zeros_like(x[:1]), x[:-1]], axis=0)


def up(x):
    return jnp.concatenate([x[1:], jnp.zeros_like(x[:1])], axis=0)


def right(x):
    rolled = pltpu.roll(x, 1, 1)
    return jnp.where(iota(x.shape, 1) == 0, 0.0, rolled)


def left(x):
    n = x.shape[1]
    rolled = pltpu.roll(x, n - 1, 1)
    return jnp.where(iota(x.shape, 1) == n - 1, 0.0, rolled)


def expand(products, fine, before, after):
    out = []
    for q in range(fine):
        t0, t1, t2 = products[q]
        prev = products[q - 1][0] if q > 0 else before(products[fine - 1][0])
        nxt = products[q + 1][2] if q < fine - 1 else after(products[0][2])
        out.append(prev + (t1 + t2))
        out.append((t0 + t1) + nxt)
    return out


def conv_up(taps, fine):
    by_col = [
        [
            expand(
                [[taps[py][px][3 * dy + dx] for dy in range(3)] for py in range(fine)],
                fine,
                down,
                up,
            )
            for dx in range(3)
        ]
        for px in range(fine)
    ]
    return [
        expand(
            [[by_col[px][dx][qy] for dx in range(3)] for px in range(fine)],
            fine,
            right,
            left,
        )
        for qy in range(2 * fine)
    ]


def segment_sum(x, block):
    count = x.shape[1] // 128
    rows = jnp.concatenate([x[:, k * 128 : (k + 1) * 128] for k in range(count)], axis=0)
    top = rows.astype(BF16)
    rest = rows - top.astype(F32)
    mid = rest.astype(BF16)
    low = (rest - mid.astype(F32)).astype(BF16)
    n = rows.shape[0]
    got = dot(jnp.concatenate([top, mid, low], axis=0), block)
    got = got[:n] + got[n : 2 * n] + got[2 * n :]
    sums = [jnp.sum(got[8 * k : 8 * k + 8], axis=0, keepdims=True) for k in range(count)]
    return jnp.concatenate(sums, axis=1) if count > 1 else sums[0]


def group_silu(phases):
    channels = phases[0].shape[-1]
    width = channels // NGROUPS
    positions = len(phases) * phases[0].shape[0] * phases[0].shape[1]
    scale = 1.0 / (positions * width)
    block = (iota((128, 128), 0) // width == iota((128, 128), 1) // width).astype(F32)
    block = block.astype(BF16)
    total = jnp.sum(functools.reduce(jnp.add, phases), axis=0)
    center = (segment_sum(total, block) * scale)[None]
    shifted = [p - center for p in phases]
    squares = jnp.sum(functools.reduce(jnp.add, [s * s for s in shifted]), axis=0)
    spread = segment_sum(squares, block) * scale
    factor = (0.5 * lax.rsqrt(spread + 1e-06))[None]
    result = []
    for s in shifted:
        half = s * factor
        result.append(half + half * jnp.tanh(half))
    return result


def table_rows(table, limits, index, count, margin, inner):
    size = table.shape[1]
    pos = iota((1, size), 1)
    far = jnp.maximum(jnp.maximum(margin - pos, pos - (margin + inner) + 1), 0)
    rows = []
    for d in (-1, 0, 1):
        here = index + d
        limit = limits[jnp.clip(here, 0, count - 1)]
        picked = jnp.where(iota(table.shape, 0) == here, table, 0.0)
        row = jnp.sum(picked, axis=0, keepdims=True)
        rows.append(jnp.where(far <= limit, row, 0.0))
    above, own, below = rows
    other = jnp.where(pos < inner, jnp.roll(above, inner, 1), jnp.roll(below, inner, 1))
    pair = jnp.concatenate([own, own + other, jnp.zeros((6, size), F32)], axis=0)
    return pair.astype(BF16)


def kernel(
    nr, nc, lat, w_in, w_mid, w_low, w_out, ramp_r, ramp_c, lim_r, lim_c, out,
    cells, wi, wm, wl, wo, tr, tc, lr, lc, wi32, wo32, own, side_out, vert_out, sides, corners, verts,
    local_sem, send1, recv1, send2, recv2,
):
    row, col = lax.axis_index("rows"), lax.axis_index("cols")

    def exists(dr, dc):
        ok = None
        for d, here, n in ((dr, row, nr), (dc, col, nc)):
            test = None if d == 0 else (here > 0 if d < 0 else here < n - 1)
            if test is not None:
                ok = test if ok is None else jnp.logical_and(ok, test)
        return ok

    def device(dr, dc):
        return {"rows": row + dr, "cols": col + dc}

    loads = [
        pltpu.make_async_copy(src, dst, local_sem.at[k])
        for k, (src, dst) in enumerate(
            [
                (lat, cells.at[4]),
                (w_in, wi),
                (ramp_r, tr),
                (ramp_c, tc),
                (lim_r, lr),
                (lim_c, lc),
                (w_mid, wm),
                (w_low, wl),
                (w_out, wo),
            ]
        )
    ]
    barrier = pltpu.get_barrier_semaphore()
    for _, (dr, dc) in FAR_FIRST:

        @pl.when(exists(dr, dc))
        def _():
            pl.semaphore_signal(barrier, inc=1, device_id=device(dr, dc), device_id_type=MESH)

    for load in loads:
        load.start()

    def slot_of(dr, dc):
        up_down, left_right = (dr + 1) // 2, (dc + 1) // 2
        if dr == 0:
            return sides.at[left_right]
        return verts.at[up_down] if dc == 0 else corners.at[left_right, up_down]

    def packed(dr, dc):
        up_down, left_right = (dr + 1) // 2, (dc + 1) // 2
        if dr == 0:
            return side_out.at[left_right]
        return vert_out.at[up_down] if dc == 0 else side_out.at[left_right, up_down]

    def copies(k, dr, dc):
        first = pltpu.make_async_remote_copy(
            src_ref=cells.at[4],
            dst_ref=cells.at[(1 - dr) * 3 + 1 - dc],
            send_sem=send1.at[k],
            recv_sem=recv1.at[7 - k],
            device_id=device(dr, dc),
            device_id_type=MESH,
        )
        second = pltpu.make_async_remote_copy(
            src_ref=packed(dr, dc),
            dst_ref=slot_of(-dr, -dc),
            send_sem=send2.at[k],
            recv_sem=recv2.at[7 - k],
            device_id=device(dr, dc),
            device_id_type=MESH,
        )
        return first, second

    def arrival(k, dr, dc):
        first = pltpu.make_async_remote_copy(
            src_ref=cells.at[4],
            dst_ref=cells.at[(1 + dr) * 3 + 1 + dc],
            send_sem=send1.at[k],
            recv_sem=recv1.at[k],
            device_id=device(dr, dc),
            device_id_type=MESH,
        )
        second = pltpu.make_async_remote_copy(
            src_ref=packed(dr, dc),
            dst_ref=slot_of(dr, dc),
            send_sem=send2.at[k],
            recv_sem=recv2.at[k],
            device_id=device(dr, dc),
            device_id_type=MESH,
        )
        return first, second

    for k, (dr, dc) in enumerate(AROUND):

        @pl.when(jnp.logical_not(exists(dr, dc)))
        def _():
            slot = cells.at[(1 + dr) * 3 + 1 + dc]
            slot[...] = jnp.zeros(slot.shape, BF16)
            pixels = slot_of(dr, dc)
            pixels[...] = jnp.zeros(pixels.shape, F32)

    neighbours = (1 + (row > 0).astype(jnp.int32) + (row < nr - 1).astype(jnp.int32)) * (
        1 + (col > 0).astype(jnp.int32) + (col < nc - 1).astype(jnp.int32)
    ) - 1
    loads[0].wait()
    pl.semaphore_wait(barrier, neighbours)
    for k, (dr, dc) in FAR_FIRST:

        @pl.when(exists(dr, dc))
        def _():
            copies(k, dr, dc)[0].start()

    loads[1].wait()
    wi32[...] = jnp.zeros(wi32.shape, F32)
    wi32[:, 0 : wi.shape[1], :] = wi[...].astype(F32)
    loads[8].wait()
    wo32[...] = jnp.zeros(wo32.shape, F32)
    wo32[:, 0 : wo.shape[1], :] = wo[...].astype(F32)
    for k in (2, 3, 4, 5):
        loads[k].wait()

    tile = lat.shape[1]
    side_cells = tile + 2 * HALO
    margin, inner = 4 * HALO, 4 * tile
    size = inner + 2 * margin
    chans = lat.shape[0]

    span = size * side_cells
    spread_r = (iota((size, span), 1) // side_cells == iota((size, span), 0)).astype(F32)
    spread_c = [
        (4 * (iota((size, span), 1) % side_cells) + q == iota((size, span), 0)).astype(F32)
        for q in range(4)
    ]
    spread_c = jnp.concatenate(spread_c, axis=1)
    row_w = dot(table_rows(tr[...].astype(F32), lr, row, nr, margin, inner), spread_r.astype(BF16))
    col_w = dot(table_rows(tc[...].astype(F32), lc, col, nc, margin, inner), spread_c.astype(BF16))
    lane = iota((1, span), 1)
    r_of, b_of = lane // side_cells, lane % side_cells
    inside = (
        (r_of >= margin) & (r_of < margin + inner) & (b_of >= HALO) & (b_of < HALO + tile)
    )
    blend, inverse = [], []
    for q in range(4):
        cw = col_w[:, q * span : (q + 1) * span]
        blend.append(row_w[0:1] * cw[0:1])
        inverse.append(1.0 / jnp.where(inside, row_w[1:2] * cw[1:2], 1.0))

    wide = chans * side_cells
    src, dst = iota((3 * wide, 72), 0), iota((3 * wide, 72), 1)
    pick = [
        (
            (dst // 8 == 3 * (src // wide) + dx)
            & (dst % 8 == (src // side_cells) % chans)
        ).astype(F32).astype(BF16)
        for dx in range(3)
    ]
    wi72 = wi32[...].reshape(72, wi32.shape[2]).astype(BF16)

    for k, (dr, dc) in enumerate(AROUND):

        @pl.when(exists(dr, dc))
        def _():
            arrival(k, dr, dc)[0].wait_recv()

    cell = [[cells[3 * i + j].astype(F32) for j in range(3)] for i in range(3)]
    bands = [
        jnp.concatenate([cell[0][j][:, tile - HALO :], cell[1][j], cell[2][j][:, :HALO]], axis=1)
        for j in range(3)
    ]
    grid = jnp.concatenate([bands[0][:, :, tile - HALO :], bands[1], bands[2][:, :, :HALO]], axis=2)
    flat = jnp.concatenate([grid[c] for c in range(chans)], axis=1)
    zero = jnp.zeros((1, wide), F32)
    tall = jnp.concatenate(
        [
            jnp.concatenate([zero, flat[:-1]], axis=0),
            flat,
            jnp.concatenate([flat[1:], zero], axis=0),
        ],
        axis=1,
    )
    shape = (side_cells, side_cells, 3 * wide)
    spreaded = jnp.broadcast_to(tall[:, None, :], shape)
    gap = iota(shape, 2) % side_cells - iota(shape, 1)
    patches = 0.0
    for dx in range(3):
        chosen = jnp.where(gap == dx - 1, spreaded, 0.0)
        patches = patches + dot(chosen.reshape(-1, 3 * wide).astype(BF16), pick[dx])
    first = dot(patches.astype(BF16), wi72).reshape(side_cells, side_cells, -1)
    (first,) = group_silu([first])
    first = first.reshape(side_cells * side_cells, -1).astype(BF16)

    loads[6].wait()
    taps = [nt_dot(first, wm[t]).reshape(side_cells, side_cells, -1) for t in range(9)]
    second = conv_up([[taps]], 1)
    second = group_silu([second[py][px] for py in range(2) for px in range(2)])
    second = jnp.concatenate(second, axis=0)
    second = second.reshape(-1, second.shape[2]).astype(BF16)

    loads[7].wait()
    n = side_cells * side_cells
    products = [nt_dot(second, wl[t]) for t in range(9)]
    taps = [
        [
            [
                p[(2 * py + px) * n : (2 * py + px + 1) * n].reshape(side_cells, side_cells, -1)
                for p in products
            ]
            for px in range(2)
        ]
        for py in range(2)
    ]
    third = conv_up(taps, 2)
    third = group_silu([third[qy][qx] for qy in range(4) for qx in range(4)])

    wo72 = wo32[...].reshape(72, wo32.shape[2]).astype(BF16)
    colour = []
    for qx in range(4):
        rows = jnp.stack([third[4 * qy + qx] for qy in range(4)], axis=1)
        colour.append(nt_dot(wo72, rows.reshape(span, rows.shape[-1]).astype(BF16)))

    def tap(q, t):
        return colour[q][8 * t : 8 * t + 8]

    half = span // 2
    where_b = iota((4, half), 1) % side_cells
    lower_half = iota((4, half), 1) < half // 2
    sub_b = iota((8, span), 1) % side_cells
    sub_r = iota((8, span), 1) // side_cells
    for q in range(4):
        by_row = []
        for dy in range(3):
            if q > 0:
                before = tap(q - 1, 3 * dy)
            else:
                before = jnp.where(sub_b == 0, 0.0, pltpu.roll(tap(3, 3 * dy), 1, 1))
            if q < 3:
                after = tap(q + 1, 3 * dy + 2)
            else:
                after = jnp.where(
                    sub_b == side_cells - 1, 0.0, pltpu.roll(tap(0, 3 * dy + 2), span - 1, 1)
                )
            by_row.append(before + tap(q, 3 * dy + 1) + after)
        value = (
            jnp.where(sub_r == 0, 0.0, pltpu.roll(by_row[0], side_cells, 1))
            + by_row[1]
            + jnp.where(sub_r == size - 1, 0.0, pltpu.roll(by_row[2], span - side_cells, 1))
        ) * blend[q]
        for h in range(2):
            own[h, q] = value[0:4, h * half : (h + 1) * half]

    for h in range(2):
        for k, rim in ((0, 0), (1, side_cells - HALO)):
            dense = pltpu.roll(own[h, 0], (half - rim) % half, 1)
            for q in range(1, 4):
                moved = pltpu.roll(own[h, q], (HALO * q - rim) % half, 1)
                dense = jnp.where(where_b // HALO == q, moved, dense)
            side_out[k, h] = dense
        for pair in range(2):
            even, odd = own[h, 2 * pair], own[h, 2 * pair + 1]
            if h == 0:
                odd = pltpu.roll(odd, half // 2, 1)
            else:
                even = pltpu.roll(even, half // 2, 1)
            vert_out[h, pair] = jnp.where(lower_half, even, odd)

    for k, (dr, dc) in FAR_FIRST:

        @pl.when(exists(dr, dc))
        def _():
            copies(k, dr, dc)[1].start()

    place_src, place_dst = iota((4 * half, inner), 0), iota((4 * half, inner), 1)
    place = (place_dst == 4 * (place_src % side_cells - HALO) + place_src // half)
    place = place.astype(F32).astype(BF16)
    lane_row = iota((8, half), 1) // side_cells
    sublane = iota((8, half), 0)
    keep = [lane_row == sublane + 8, lane_row == sublane]

    for k, (dr, dc) in enumerate(AROUND):

        @pl.when(exists(dr, dc))
        def _():
            arrival(k, dr, dc)[1].wait_recv()

    blocks = [[], [], []]
    for h in range(2):
        pieces = []
        lft = sides[0, h] + corners[0, h]
        rgt = sides[1, h] + corners[1, h]
        for q in range(4):
            beyond = verts[h, q // 2]
            if (q + h) % 2 == 0:
                beyond = pltpu.roll(beyond, half // 2, 1)
            lft_q = pltpu.roll(lft, (HALO - HALO * q) % half, 1)
            rgt_q = pltpu.roll(rgt, (tile - HALO * q) % half, 1)
            mid = own[h, q] + beyond + jnp.where(where_b < side_cells // 2, lft_q, rgt_q)
            pieces.append(mid * inverse[q][:, h * half : (h + 1) * half])
        for c in range(3):
            spread_rows = [
                jnp.where(keep[h], jnp.broadcast_to(p[c : c + 1], (8, half)), 0.0) for p in pieces
            ]
            blocks[c].append(jnp.concatenate(spread_rows, axis=1))
    tall = jnp.concatenate([b for c in range(3) for b in blocks[c]], axis=0)
    top = tall.astype(BF16)
    low = (tall - top.astype(F32)).astype(BF16)
    image = dot(top, place) + dot(low, place)
    out[...] = image.reshape(3, inner, inner)

    for k, (dr, dc) in enumerate(AROUND):

        @pl.when(exists(dr, dc))
        def _():
            for copy in copies(k, dr, dc):
                copy.wait_send()


def solution(mesh):
    nr, nc = mesh.shape["rows"], mesh.shape["cols"]

    def per_device(lat, w_in, w_mid, w_low, w_out, ramp_r, ramp_c, lim_r, lim_c):
        tile = lat.shape[1]
        inner = 4 * tile
        size = inner + 8 * HALO
        half = size * (tile + 2 * HALO) // 2
        anywhere = pl.BlockSpec(memory_space=pltpu.HBM)
        dma = pltpu.SemaphoreType.DMA
        return pl.pallas_call(
            functools.partial(kernel, nr, nc),
            out_shape=pltpu.VMEM((w_out.shape[1], inner, inner), F32),
            in_specs=[anywhere] * 9,
            out_specs=pl.BlockSpec(memory_space=pltpu.VMEM),
            scratch_shapes=[
                pltpu.VMEM((9,) + lat.shape, BF16),
                pltpu.VMEM(w_in.shape, BF16),
                pltpu.VMEM(w_mid.shape, BF16),
                pltpu.VMEM(w_low.shape, BF16),
                pltpu.VMEM(w_out.shape, BF16),
                pltpu.VMEM(ramp_r.shape, jnp.int32),
                pltpu.VMEM(ramp_c.shape, jnp.int32),
                pltpu.SMEM(lim_r.shape, jnp.int32),
                pltpu.SMEM(lim_c.shape, jnp.int32),
                pltpu.VMEM((9, 8, w_in.shape[2]), F32),
                pltpu.VMEM((9, 8, w_out.shape[2]), F32),
                pltpu.VMEM((2, 4, 4, half), F32),
                pltpu.VMEM((2, 2, 4, half), F32),
                pltpu.VMEM((2, 2, 4, half), F32),
                pltpu.VMEM((2, 2, 4, half), F32),
                pltpu.VMEM((2, 2, 4, half), F32),
                pltpu.VMEM((2, 2, 4, half), F32),
                dma((9,)),
                dma((8,)),
                dma((8,)),
                dma((8,)),
                dma((8,)),
            ],
            compiler_params=pltpu.CompilerParams(
                collective_id=0, has_side_effects=True
            ),
            name="decode",
        )(lat, w_in, w_mid, w_low, w_out, ramp_r, ramp_c, lim_r, lim_c)

    return jax.shard_map(
        per_device,
        mesh=mesh,
        in_specs=(P(None, ("groups", "rows"), "cols"), P(), P(), P(), P(), P(), P(), P(), P()),
        out_specs=P(None, ("groups", "rows"), "cols"),
        check_vma=False,
    )
```

profile of v0, /device:TPU:1, one launch (start us, length us, event | category | flops | bytes accessed | tf_op | source)
XLA Modules:
  0.0 14.7 jit_solution(5570638310519283940)
XLA Ops:
  0.0 14.1 %decode.1 = f32[3,16,16]{2,1,0:T(8,128)S(1)} custom-call(bf16[4,4,4]{2,1,0:T(4,128)(2,1)} %lat.1, bf16[9,4,512]{2,1,0:T(4,128)(2,1)} %w_in.1, bf16[9,256,512]{2,1,0:T(8,128)(2,1)} %w_mid.1, bf16[9,128,256]{2,1,0:T(8,128)(2,1)} %w_low.1, bf16[9,3,128]{2,1,0:T(4,128)(2,1)} %w_out.1, s32[4,32]{1,0:T(4,128)} %ramp_r.1, s32[4,32]{1,0:T(4,128)} %ramp_c.1, ...), custom_call_target="tpu_custom_call" | custom-call | tf_op jit(solution)/shard_map/decode/pallas_call | solution.py:464
  14.1 0.6 %copy.11 = f32[3,16,16]{2,1,0:T(8,128)} copy(f32[3,16,16]{2,1,0:T(8,128)S(1)} %decode.1) | data formatting | bytes 6144
where the time goes:
time: 14.8 us; the launch traced here: 14.7 us
  Pallas kernels  14.1 us (95%)
  local copies, waits for them, and re-layouts  0.61 us (4%)
    pallas_call x1, Pallas kernels, per_device(): pl.pallas_call(functools.partial(kernel, nr, nc), out_shape=pltpu.VMEM((w...  14.1 us
    unnamed x1, local copies, waits for them, and re-layouts  0.61 us

commit v1 on v0

--- a/solution.py
+++ b/solution.py
@@ -14,6 +14,8 @@
 BF16 = jnp.bfloat16
 AROUND = [(dr, dc) for dr in (-1, 0, 1) for dc in (-1, 0, 1) if (dr, dc) != (0, 0)]
 FAR_FIRST = sorted(enumerate(AROUND), key=lambda e: -abs(e[1][0]) - abs(e[1][1]))
+EARLIER = [(k, *to) for k, to in FAR_FIRST if k < 4]
+LATER = [(k, *to) for k, to in FAR_FIRST if k >= 4]
 
 
 def iota(shape, dim):
@@ -136,7 +138,7 @@
 def kernel(
     nr, nc, lat, w_in, w_mid, w_low, w_out, ramp_r, ramp_c, lim_r, lim_c, out,
     cells, wi, wm, wl, wo, tr, tc, lr, lc, wi32, wo32, own, side_out, vert_out, sides, corners, verts,
-    local_sem, send1, recv1, send2, recv2,
+    local_sem, ready, send1, recv1, send2, recv2,
 ):
     row, col = lax.axis_index("rows"), lax.axis_index("cols")
 
@@ -167,15 +169,15 @@
             ]
         )
     ]
-    barrier = pltpu.get_barrier_semaphore()
-    for _, (dr, dc) in FAR_FIRST:
-
-        @pl.when(exists(dr, dc))
-        def _():
-            pl.semaphore_signal(barrier, inc=1, device_id=device(dr, dc), device_id_type=MESH)
-
     for load in loads:
         load.start()
+
+    barrier = pltpu.get_barrier_semaphore()
+    for k, dr, dc in LATER:
+
+        @pl.when(exists(dr, dc))
+        def _():
+            pl.semaphore_signal(barrier, inc=1, device_id=device(dr, dc), device_id_type=MESH)
 
     def slot_of(dr, dc):
         up_down, left_right = (dr + 1) // 2, (dc + 1) // 2
@@ -236,17 +238,38 @@
             pixels = slot_of(dr, dc)
             pixels[...] = jnp.zeros(pixels.shape, F32)
 
-    neighbours = (1 + (row > 0).astype(jnp.int32) + (row < nr - 1).astype(jnp.int32)) * (
+    earlier = (col > 0).astype(jnp.int32) + (row > 0).astype(jnp.int32) * (
         1 + (col > 0).astype(jnp.int32) + (col < nc - 1).astype(jnp.int32)
-    ) - 1
+    )
+
+    @pl.when(row + col > 0)
+    def _():
+        pl.semaphore_wait(barrier, earlier)
+
+    for k, dr, dc in EARLIER:
+
+        @pl.when(exists(dr, dc))
+        def _():
+            pl.semaphore_signal(
+                ready.at[3 - k], inc=1, device_id=device(dr, dc), device_id_type=MESH
+            )
+
     loads[0].wait()
-    pl.semaphore_wait(barrier, neighbours)
-    for k, (dr, dc) in FAR_FIRST:
+    for k, dr, dc in EARLIER:
 
         @pl.when(exists(dr, dc))
         def _():
             copies(k, dr, dc)[0].start()
 
+    def send_later(entries):
+        for k, dr, dc in entries:
+
+            @pl.when(exists(dr, dc))
+            def _():
+                pl.semaphore_wait(ready.at[k - 4], 1)
+                copies(k, dr, dc)[0].start()
+
+    send_later([e for e in LATER if e[1] == 0])
     loads[1].wait()
     wi32[...] = jnp.zeros(wi32.shape, F32)
     wi32[:, 0 : wi.shape[1], :] = wi[...].astype(F32)
@@ -293,6 +316,7 @@
     ]
     wi72 = wi32[...].reshape(72, wi32.shape[2]).astype(BF16)
 
+    send_later([e for e in LATER if e[1] != 0])
     for k, (dr, dc) in enumerate(AROUND):
 
         @pl.when(exists(dr, dc))
@@ -485,6 +509,7 @@
                 pltpu.VMEM((2, 2, 4, half), F32),
                 pltpu.VMEM((2, 2, 4, half), F32),
                 dma((9,)),
+                pltpu.SemaphoreType.REGULAR((4,)),
                 dma((8,)),
                 dma((8,)),
                 dma((8,)),

time: 14.8 us -> 14.6 us (0.986)
  Pallas kernels: 14.1 us -> 13.8 us
    pallas_call x1, Pallas kernels: 14.1 us -> 13.8 us  [per_device(): pl.pallas_call(functools.partial(kernel, nr, nc), out_shape=pltpu.VMEM((w...]
where the time goes in v1:
time: 14.6 us; the launch traced here: 14.4 us
  Pallas kernels  13.8 us (95%)
  local copies, waits for them, and re-layouts  0.61 us (4%)
    pallas_call x1, Pallas kernels, per_device(): pl.pallas_call(functools.partial(kernel, nr, nc), out_shape=pltpu.VMEM((w...  13.8 us
    unnamed x1, local copies, waits for them, and re-layouts  0.61 us

profile of v1, /device:TPU:1, one launch (start us, length us, event | category | flops | bytes accessed | tf_op | source)
XLA Modules:
  0.0 14.4 jit_solution(4349144521884857674)
XLA Ops:
  0.0 13.8 %decode.1 = f32[3,16,16]{2,1,0:T(8,128)S(1)} custom-call(bf16[4,4,4]{2,1,0:T(4,128)(2,1)} %lat.1, bf16[9,4,512]{2,1,0:T(4,128)(2,1)} %w_in.1, bf16[9,256,512]{2,1,0:T(8,128)(2,1)} %w_mid.1, bf16[9,128,256]{2,1,0:T(8,128)(2,1)} %w_low.1, bf16[9,3,128]{2,1,0:T(4,128)(2,1)} %w_out.1, s32[4,32]{1,0:T(4,128)} %ramp_r.1, s32[4,32]{1,0:T(4,128)} %ramp_c.1, ...), custom_call_target="tpu_custom_call" | custom-call | tf_op jit(solution)/shard_map/decode/pallas_call | solution.py:488
  13.8 0.6 %copy.11 = f32[3,16,16]{2,1,0:T(8,128)} copy(f32[3,16,16]{2,1,0:T(8,128)S(1)} %decode.1) | data formatting | bytes 6144

commit v2 on v1

--- a/solution.py
+++ b/solution.py
@@ -15,7 +15,7 @@
 AROUND = [(dr, dc) for dr in (-1, 0, 1) for dc in (-1, 0, 1) if (dr, dc) != (0, 0)]
 FAR_FIRST = sorted(enumerate(AROUND), key=lambda e: -abs(e[1][0]) - abs(e[1][1]))
 EARLIER = [(k, *to) for k, to in FAR_FIRST if k < 4]
-LATER = [(k, *to) for k, to in FAR_FIRST if k >= 4]
+LATER = [(k, *AROUND[k]) for k in range(4, 8)]
 
 
 def iota(shape, dim):
@@ -84,36 +84,33 @@
     ]
 
 
-def segment_sum(x, block):
-    count = x.shape[1] // 128
-    rows = jnp.concatenate([x[:, k * 128 : (k + 1) * 128] for k in range(count)], axis=0)
+def group_silu(phases):
+    channels = phases[0].shape[-1]
+    width = channels // NGROUPS
+    count = channels // 128
+    positions = len(phases) * phases[0].shape[0] * phases[0].shape[1]
+    scale = 1.0 / (positions * width)
+    block = (iota((384, 128), 0) % 128 // width == iota((384, 128), 1) // width).astype(F32)
+    block = block.astype(BF16)
+    total = jnp.sum(functools.reduce(jnp.add, phases), axis=(0, 1)).reshape(1, channels)
+    squares = functools.reduce(jnp.add, [p * p for p in phases])
+    squares = jnp.sum(squares, axis=(0, 1)).reshape(1, channels)
+    rows = [x[:, k * 128 : (k + 1) * 128] for x in (total, squares) for k in range(count)]
+    rows = jnp.concatenate(rows + [jnp.zeros((1, 128), F32)] * (8 - len(rows)), axis=0)
     top = rows.astype(BF16)
     rest = rows - top.astype(F32)
     mid = rest.astype(BF16)
     low = (rest - mid.astype(F32)).astype(BF16)
-    n = rows.shape[0]
-    got = dot(jnp.concatenate([top, mid, low], axis=0), block)
-    got = got[:n] + got[n : 2 * n] + got[2 * n :]
-    sums = [jnp.sum(got[8 * k : 8 * k + 8], axis=0, keepdims=True) for k in range(count)]
-    return jnp.concatenate(sums, axis=1) if count > 1 else sums[0]
-
-
-def group_silu(phases):
-    channels = phases[0].shape[-1]
-    width = channels // NGROUPS
-    positions = len(phases) * phases[0].shape[0] * phases[0].shape[1]
-    scale = 1.0 / (positions * width)
-    block = (iota((128, 128), 0) // width == iota((128, 128), 1) // width).astype(F32)
-    block = block.astype(BF16)
-    total = jnp.sum(functools.reduce(jnp.add, phases), axis=0)
-    center = (segment_sum(total, block) * scale)[None]
-    shifted = [p - center for p in phases]
-    squares = jnp.sum(functools.reduce(jnp.add, [s * s for s in shifted]), axis=0)
-    spread = segment_sum(squares, block) * scale
-    factor = (0.5 * lax.rsqrt(spread + 1e-06))[None]
+    got = dot(jnp.concatenate([top, mid, low], axis=1), block) * scale
+    center = got[:count]
+    spread = jnp.maximum(got[count : 2 * count] - center * center, 0.0)
+    factor = 0.5 * lax.rsqrt(spread + 1e-06)
+    offset = center * factor
+    factor = jnp.concatenate([factor[k : k + 1] for k in range(count)], axis=1)[None]
+    offset = jnp.concatenate([offset[k : k + 1] for k in range(count)], axis=1)[None]
     result = []
-    for s in shifted:
-        half = s * factor
+    for p in phases:
+        half = p * factor - offset
         result.append(half + half * jnp.tanh(half))
     return result
 
@@ -137,7 +134,7 @@
 
 def kernel(
     nr, nc, lat, w_in, w_mid, w_low, w_out, ramp_r, ramp_c, lim_r, lim_c, out,
-    cells, wi, wm, wl, wo, tr, tc, lr, lc, wi32, wo32, own, side_out, vert_out, sides, corners, verts,
+    cells, wi, wm, wl, wo, tr, tc, lr, lc, wi32, wo32, own, side_out, vert_out, rims,
     local_sem, ready, send1, recv1, send2, recv2,
 ):
     row, col = lax.axis_index("rows"), lax.axis_index("cols")
@@ -163,9 +160,9 @@
                 (ramp_c, tc),
                 (lim_r, lr),
                 (lim_c, lc),
+                (w_out, wo),
                 (w_mid, wm),
                 (w_low, wl),
-                (w_out, wo),
             ]
         )
     ]
@@ -182,8 +179,10 @@
     def slot_of(dr, dc):
         up_down, left_right = (dr + 1) // 2, (dc + 1) // 2
         if dr == 0:
-            return sides.at[left_right]
-        return verts.at[up_down] if dc == 0 else corners.at[left_right, up_down]
+            return rims.at[pl.ds(2 * left_right, 2)]
+        if dc == 0:
+            return rims.at[pl.ds(8 + 2 * up_down, 2)]
+        return rims.at[4 + 2 * left_right + up_down]
 
     def packed(dr, dc):
         up_down, left_right = (dr + 1) // 2, (dc + 1) // 2
@@ -195,39 +194,44 @@
         first = pltpu.make_async_remote_copy(
             src_ref=cells.at[4],
             dst_ref=cells.at[(1 - dr) * 3 + 1 - dc],
-            send_sem=send1.at[k],
-            recv_sem=recv1.at[7 - k],
+            send_sem=send1,
+            recv_sem=recv1,
             device_id=device(dr, dc),
             device_id_type=MESH,
         )
         second = pltpu.make_async_remote_copy(
             src_ref=packed(dr, dc),
             dst_ref=slot_of(-dr, -dc),
-            send_sem=send2.at[k],
-            recv_sem=recv2.at[7 - k],
+            send_sem=send2,
+            recv_sem=recv2,
             device_id=device(dr, dc),
             device_id_type=MESH,
         )
         return first, second
 
-    def arrival(k, dr, dc):
-        first = pltpu.make_async_remote_copy(
-            src_ref=cells.at[4],
-            dst_ref=cells.at[(1 + dr) * 3 + 1 + dc],
-            send_sem=send1.at[k],
-            recv_sem=recv1.at[k],
-            device_id=device(dr, dc),
+    above_below = (row > 0).astype(jnp.int32) + (row < nr - 1).astype(jnp.int32)
+    beside = (col > 0).astype(jnp.int32) + (col < nc - 1).astype(jnp.int32)
+
+    def for_all(wait):
+        for v in range(min(nr, 2) - 1, min(nr, 3)):
+            for h in range(min(nc, 2) - 1, min(nc, 3)):
+                if v + h == 0:
+                    continue
+
+                @pl.when(jnp.logical_and(above_below == v, beside == h))
+                def _():
+                    wait(v + h + v * h, 2 * (v + h) + v * h)
+
+    def batch(ref, n, send, recv):
+        part = ref.at[pl.ds(0, n)]
+        return pltpu.make_async_remote_copy(
+            src_ref=part,
+            dst_ref=part,
+            send_sem=send,
+            recv_sem=recv,
+            device_id=device(0, 0),
             device_id_type=MESH,
         )
-        second = pltpu.make_async_remote_copy(
-            src_ref=packed(dr, dc),
-            dst_ref=slot_of(dr, dc),
-            send_sem=send2.at[k],
-            recv_sem=recv2.at[k],
-            device_id=device(dr, dc),
-            device_id_type=MESH,
-        )
-        return first, second
 
     for k, (dr, dc) in enumerate(AROUND):
 
@@ -269,11 +273,11 @@
                 pl.semaphore_wait(ready.at[k - 4], 1)
                 copies(k, dr, dc)[0].start()
 
-    send_later([e for e in LATER if e[1] == 0])
+    send_later(LATER)
     loads[1].wait()
     wi32[...] = jnp.zeros(wi32.shape, F32)
     wi32[:, 0 : wi.shape[1], :] = wi[...].astype(F32)
-    loads[8].wait()
+    loads[6].wait()
     wo32[...] = jnp.zeros(wo32.shape, F32)
     wo32[:, 0 : wo.shape[1], :] = wo[...].astype(F32)
     for k in (2, 3, 4, 5):
@@ -316,12 +320,7 @@
     ]
     wi72 = wi32[...].reshape(72, wi32.shape[2]).astype(BF16)
 
-    send_later([e for e in LATER if e[1] != 0])
-    for k, (dr, dc) in enumerate(AROUND):
-
-        @pl.when(exists(dr, dc))
-        def _():
-            arrival(k, dr, dc)[0].wait_recv()
+    for_all(lambda n, m: batch(cells, n, send1, recv1).wait_recv())
 
     cell = [[cells[3 * i + j].astype(F32) for j in range(3)] for i in range(3)]
     bands = [
@@ -350,16 +349,17 @@
     (first,) = group_silu([first])
     first = first.reshape(side_cells * side_cells, -1).astype(BF16)
 
-    loads[6].wait()
+    loads[7].wait()
     taps = [nt_dot(first, wm[t]).reshape(side_cells, side_cells, -1) for t in range(9)]
     second = conv_up([[taps]], 1)
     second = group_silu([second[py][px] for py in range(2) for px in range(2)])
     second = jnp.concatenate(second, axis=0)
     second = second.reshape(-1, second.shape[2]).astype(BF16)
 
-    loads[7].wait()
+    loads[8].wait()
     n = side_cells * side_cells
-    products = [nt_dot(second, wl[t]) for t in range(9)]
+    products = nt_dot(second, wl[...].reshape(-1, wl.shape[2]))
+    products = [products[:, wl.shape[1] * t : wl.shape[1] * (t + 1)] for t in range(9)]
     taps = [
         [
             [
@@ -437,19 +437,15 @@
     sublane = iota((8, half), 0)
     keep = [lane_row == sublane + 8, lane_row == sublane]
 
-    for k, (dr, dc) in enumerate(AROUND):
-
-        @pl.when(exists(dr, dc))
-        def _():
-            arrival(k, dr, dc)[1].wait_recv()
+    for_all(lambda n, m: batch(rims, m, send2, recv2).wait_recv())
 
     blocks = [[], [], []]
     for h in range(2):
         pieces = []
-        lft = sides[0, h] + corners[0, h]
-        rgt = sides[1, h] + corners[1, h]
+        lft = rims[h] + rims[4 + h]
+        rgt = rims[2 + h] + rims[6 + h]
         for q in range(4):
-            beyond = verts[h, q // 2]
+            beyond = rims[8 + 2 * h + q // 2]
             if (q + h) % 2 == 0:
                 beyond = pltpu.roll(beyond, half // 2, 1)
             lft_q = pltpu.roll(lft, (HALO - HALO * q) % half, 1)
@@ -467,12 +463,8 @@
     image = dot(top, place) + dot(low, place)
     out[...] = image.reshape(3, inner, inner)
 
-    for k, (dr, dc) in enumerate(AROUND):
-
-        @pl.when(exists(dr, dc))
-        def _():
-            for copy in copies(k, dr, dc):
-                copy.wait_send()
+    for_all(lambda n, m: batch(cells, n, send1, recv1).wait_send())
+    for_all(lambda n, m: batch(rims, m, send2, recv2).wait_send())
 
 
 def solution(mesh):
@@ -505,15 +497,13 @@
                 pltpu.VMEM((2, 4, 4, half), F32),
                 pltpu.VMEM((2, 2, 4, half), F32),
                 pltpu.VMEM((2, 2, 4, half), F32),
-                pltpu.VMEM((2, 2, 4, half), F32),
-                pltpu.VMEM((2, 2, 4, half), F32),
-                pltpu.VMEM((2, 2, 4, half), F32),
+                pltpu.VMEM((12, 4, half), F32),
                 dma((9,)),
                 pltpu.SemaphoreType.REGULAR((4,)),
-                dma((8,)),
-                dma((8,)),
-                dma((8,)),
-                dma((8,)),
+                dma,
+                dma,
+                dma,
+                dma,
             ],
             compiler_params=pltpu.CompilerParams(
                 collective_id=0, has_side_effects=True

time: 14.6 us -> 13.7 us (0.938)
  Pallas kernels: 13.8 us -> 13 us
    pallas_call x1, Pallas kernels: 13.8 us -> 13 us  [per_device(): pl.pallas_call(functools.partial(kernel, nr, nc), out_shape=pltpu.VMEM((w...]
where the time goes in v2:
time: 13.7 us; the launch traced here: 13.6 us
  Pallas kernels  13 us (95%)
  local copies, waits for them, and re-layouts  0.61 us (4%)
    pallas_call x1, Pallas kernels, per_device(): pl.pallas_call(functools.partial(kernel, nr, nc), out_shape=pltpu.VMEM((w...  13 us
    unnamed x1, local copies, waits for them, and re-layouts  0.61 us

profile of v2, /device:TPU:1, one launch (start us, length us, event | category | flops | bytes accessed | tf_op | source)
XLA Modules:
  0.0 13.6 jit_solution(11635795499196778954)
XLA Ops:
  0.0 13.0 %decode.1 = f32[3,16,16]{2,1,0:T(8,128)S(1)} custom-call(bf16[4,4,4]{2,1,0:T(4,128)(2,1)} %lat.1, bf16[9,4,512]{2,1,0:T(4,128)(2,1)} %w_in.1, bf16[9,256,512]{2,1,0:T(8,128)(2,1)} %w_mid.1, bf16[9,128,256]{2,1,0:T(8,128)(2,1)} %w_low.1, bf16[9,3,128]{2,1,0:T(4,128)(2,1)} %w_out.1, s32[4,32]{1,0:T(4,128)} %ramp_r.1, s32[4,32]{1,0:T(4,128)} %ramp_c.1, ...), custom_call_target="tpu_custom_call" | custom-call | tf_op jit(solution)/shard_map/decode/pallas_call | solution.py:480
  13.0 0.6 %copy.11 = f32[3,16,16]{2,1,0:T(8,128)} copy(f32[3,16,16]{2,1,0:T(8,128)S(1)} %decode.1) | data formatting | bytes 6144

commit v3 on v2

--- a/solution.py
+++ b/solution.py
@@ -134,7 +134,8 @@
 
 def kernel(
     nr, nc, lat, w_in, w_mid, w_low, w_out, ramp_r, ramp_c, lim_r, lim_c, out,
-    cells, wi, wm, wl, wo, tr, tc, lr, lc, wi32, wo32, own, side_out, vert_out, rims,
+    cells, wi, wm, wl, wo, tr, tc, lr, lc, wi32, wo32, wc, wmt, wlt,
+    blend, inverse, own, side_out, vert_out, rims,
     local_sem, ready, send1, recv1, send2, recv2,
 ):
     row, col = lax.axis_index("rows"), lax.axis_index("cols")
@@ -273,23 +274,31 @@
                 pl.semaphore_wait(ready.at[k - 4], 1)
                 copies(k, dr, dc)[0].start()
 
-    send_later(LATER)
-    loads[1].wait()
-    wi32[...] = jnp.zeros(wi32.shape, F32)
-    wi32[:, 0 : wi.shape[1], :] = wi[...].astype(F32)
-    loads[6].wait()
-    wo32[...] = jnp.zeros(wo32.shape, F32)
-    wo32[:, 0 : wo.shape[1], :] = wo[...].astype(F32)
-    for k in (2, 3, 4, 5):
-        loads[k].wait()
+    send_later([e for e in LATER if e[1] == 0])
 
     tile = lat.shape[1]
     side_cells = tile + 2 * HALO
     margin, inner = 4 * HALO, 4 * tile
     size = inner + 2 * margin
     chans = lat.shape[0]
-
     span = size * side_cells
+    half = span // 2
+    wide = chans * side_cells
+
+    loads[1].wait()
+    wi32[...] = jnp.zeros(wi32.shape, F32)
+    wi32[:, 0 : wi.shape[1], :] = wi[...].astype(F32)
+    wi72 = wi32[...].reshape(72, wi32.shape[2]).astype(BF16)
+    src, dst = iota((384, 72), 0), iota((384, 72), 1)
+    pick = (
+        (dst // 8 == 3 * (src % 128 // wide) + src // 128)
+        & (dst % 8 == (src // side_cells) % chans)
+        & (src % 128 < 3 * wide)
+    )
+    wc[...] = dot(pick.astype(F32).astype(BF16), wi72).astype(BF16)
+    for k in (2, 3, 4, 5):
+        loads[k].wait()
+
     spread_r = (iota((size, span), 1) // side_cells == iota((size, span), 0)).astype(F32)
     spread_c = [
         (4 * (iota((size, span), 1) % side_cells) + q == iota((size, span), 0)).astype(F32)
@@ -303,63 +312,63 @@
     inside = (
         (r_of >= margin) & (r_of < margin + inner) & (b_of >= HALO) & (b_of < HALO + tile)
     )
-    blend, inverse = [], []
     for q in range(4):
         cw = col_w[:, q * span : (q + 1) * span]
-        blend.append(row_w[0:1] * cw[0:1])
-        inverse.append(1.0 / jnp.where(inside, row_w[1:2] * cw[1:2], 1.0))
-
-    wide = chans * side_cells
-    src, dst = iota((3 * wide, 72), 0), iota((3 * wide, 72), 1)
-    pick = [
-        (
-            (dst // 8 == 3 * (src // wide) + dx)
-            & (dst % 8 == (src // side_cells) % chans)
-        ).astype(F32).astype(BF16)
-        for dx in range(3)
-    ]
-    wi72 = wi32[...].reshape(72, wi32.shape[2]).astype(BF16)
+        blend[q] = jnp.broadcast_to(row_w[0:1] * cw[0:1], (8, span))
+        inverse[q] = jnp.broadcast_to(
+            1.0 / jnp.where(inside, row_w[1:2] * cw[1:2], 1.0), (8, span)
+        )
+
+    send_later([e for e in LATER if e[1] != 0])
+
+    loads[6].wait()
+    wo32[...] = jnp.zeros(wo32.shape, F32)
+    wo32[:, 0 : wo.shape[1], :] = wo[...].astype(F32)
+    loads[7].wait()
+    out_mid = wm.shape[1]
+    for t in range(9):
+        wmt[:, out_mid * t : out_mid * (t + 1)] = wm[t].T
+    loads[8].wait()
+    out_low = wl.shape[1]
+    for t in range(9):
+        wlt[:, out_low * t : out_low * (t + 1)] = wl[t].T
 
     for_all(lambda n, m: batch(cells, n, send1, recv1).wait_recv())
 
-    cell = [[cells[3 * i + j].astype(F32) for j in range(3)] for i in range(3)]
-    bands = [
-        jnp.concatenate([cell[0][j][:, tile - HALO :], cell[1][j], cell[2][j][:, :HALO]], axis=1)
-        for j in range(3)
-    ]
-    grid = jnp.concatenate([bands[0][:, :, tile - HALO :], bands[1], bands[2][:, :, :HALO]], axis=2)
-    flat = jnp.concatenate([grid[c] for c in range(chans)], axis=1)
-    zero = jnp.zeros((1, wide), F32)
-    tall = jnp.concatenate(
-        [
-            jnp.concatenate([zero, flat[:-1]], axis=0),
-            flat,
-            jnp.concatenate([flat[1:], zero], axis=0),
-        ],
-        axis=1,
-    )
-    shape = (side_cells, side_cells, 3 * wide)
+    cell = [cells[k].astype(F32) for k in range(9)]
+    pieces = [[], [], []]
+    for c in range(chans):
+        for j, cut in enumerate((slice(tile - HALO, tile), slice(0, tile), slice(0, HALO))):
+            upper, middle, lower = (cell[3 * i + j][c][:, cut] for i in range(3))
+            zero = jnp.zeros((1, middle.shape[1]), F32)
+            upper, lower = upper[tile - HALO :], lower[:HALO]
+            pieces[0].append(jnp.concatenate([zero, upper, middle, lower[:-1]], axis=0))
+            pieces[1].append(jnp.concatenate([upper, middle, lower], axis=0))
+            pieces[2].append(jnp.concatenate([upper[1:], middle, lower, zero], axis=0))
+    pieces = pieces[0] + pieces[1] + pieces[2]
+    tall = jnp.concatenate(pieces + [jnp.zeros((side_cells, 128 - 3 * wide), F32)], axis=1)
+    shape = (side_cells, side_cells, 128)
     spreaded = jnp.broadcast_to(tall[:, None, :], shape)
     gap = iota(shape, 2) % side_cells - iota(shape, 1)
-    patches = 0.0
-    for dx in range(3):
-        chosen = jnp.where(gap == dx - 1, spreaded, 0.0)
-        patches = patches + dot(chosen.reshape(-1, 3 * wide).astype(BF16), pick[dx])
-    first = dot(patches.astype(BF16), wi72).reshape(side_cells, side_cells, -1)
+    patches = [jnp.where(gap == dx - 1, spreaded, 0.0) for dx in range(3)]
+    patches = jnp.concatenate(patches, axis=2).reshape(-1, 384).astype(BF16)
+    first = dot(patches, wc[...]).reshape(side_cells, side_cells, -1)
     (first,) = group_silu([first])
     first = first.reshape(side_cells * side_cells, -1).astype(BF16)
 
-    loads[7].wait()
-    taps = [nt_dot(first, wm[t]).reshape(side_cells, side_cells, -1) for t in range(9)]
+    taps = dot(first, wmt[...])
+    taps = [
+        taps[:, out_mid * t : out_mid * (t + 1)].reshape(side_cells, side_cells, -1)
+        for t in range(9)
+    ]
     second = conv_up([[taps]], 1)
     second = group_silu([second[py][px] for py in range(2) for px in range(2)])
     second = jnp.concatenate(second, axis=0)
     second = second.reshape(-1, second.shape[2]).astype(BF16)
 
-    loads[8].wait()
     n = side_cells * side_cells
-    products = nt_dot(second, wl[...].reshape(-1, wl.shape[2]))
-    products = [products[:, wl.shape[1] * t : wl.shape[1] * (t + 1)] for t in range(9)]
+    products = dot(second, wlt[...])
+    products = [products[:, out_low * t : out_low * (t + 1)] for t in range(9)]
     taps = [
         [
             [
@@ -382,30 +391,34 @@
     def tap(q, t):
         return colour[q][8 * t : 8 * t + 8]
 
-    half = span // 2
     where_b = iota((4, half), 1) % side_cells
     lower_half = iota((4, half), 1) < half // 2
     sub_b = iota((8, span), 1) % side_cells
     sub_r = iota((8, span), 1) // side_cells
+    row_ok = [sub_r > 0, None, sub_r < size - 1]
+    col_ok = [sub_b > 0, None, sub_b < side_cells - 1]
+
+    def moved(x, dy, dx):
+        shift = (side_cells * (1 - dy) + 1 - dx) % span
+        x = pltpu.roll(x, shift, 1) if shift else x
+        ok = [m for m in (row_ok[dy], col_ok[dx]) if m is not None]
+        return jnp.where(functools.reduce(jnp.logical_and, ok), x, 0.0) if ok else x
+
     for q in range(4):
-        by_row = []
+        value = None
         for dy in range(3):
+            near = tap(q, 3 * dy + 1)
             if q > 0:
-                before = tap(q - 1, 3 * dy)
-            else:
-                before = jnp.where(sub_b == 0, 0.0, pltpu.roll(tap(3, 3 * dy), 1, 1))
+                near = near + tap(q - 1, 3 * dy)
             if q < 3:
-                after = tap(q + 1, 3 * dy + 2)
-            else:
-                after = jnp.where(
-                    sub_b == side_cells - 1, 0.0, pltpu.roll(tap(0, 3 * dy + 2), span - 1, 1)
-                )
-            by_row.append(before + tap(q, 3 * dy + 1) + after)
-        value = (
-            jnp.where(sub_r == 0, 0.0, pltpu.roll(by_row[0], side_cells, 1))
-            + by_row[1]
-            + jnp.where(sub_r == size - 1, 0.0, pltpu.roll(by_row[2], span - side_cells, 1))
-        ) * blend[q]
+                near = near + tap(q + 1, 3 * dy + 2)
+            term = moved(near, dy, 1)
+            if q == 0:
+                term = term + moved(tap(3, 3 * dy), dy, 0)
+            if q == 3:
+                term = term + moved(tap(0, 3 * dy + 2), dy, 2)
+            value = term if value is None else value + term
+        value = value * blend[q]
         for h in range(2):
             own[h, q] = value[0:4, h * half : (h + 1) * half]
 
@@ -413,8 +426,8 @@
         for k, rim in ((0, 0), (1, side_cells - HALO)):
             dense = pltpu.roll(own[h, 0], (half - rim) % half, 1)
             for q in range(1, 4):
-                moved = pltpu.roll(own[h, q], (HALO * q - rim) % half, 1)
-                dense = jnp.where(where_b // HALO == q, moved, dense)
+                turned = pltpu.roll(own[h, q], (HALO * q - rim) % half, 1)
+                dense = jnp.where(where_b // HALO == q, turned, dense)
             side_out[k, h] = dense
         for pair in range(2):
             even, odd = own[h, 2 * pair], own[h, 2 * pair + 1]
@@ -430,38 +443,75 @@
         def _():
             copies(k, dr, dc)[1].start()
 
-    place_src, place_dst = iota((4 * half, inner), 0), iota((4 * half, inner), 1)
-    place = (place_dst == 4 * (place_src % side_cells - HALO) + place_src // half)
-    place = place.astype(F32).astype(BF16)
     lane_row = iota((8, half), 1) // side_cells
     sublane = iota((8, half), 0)
     keep = [lane_row == sublane + 8, lane_row == sublane]
+    beyond_row = [lane_row % 8 == sublane, lane_row % 8 == sublane]
+
+    def spread_rows(piece, c, mask):
+        return jnp.where(mask, jnp.broadcast_to(piece[c : c + 1], (8, half)), 0.0)
+
+    def placed(blocks, place):
+        tall = jnp.concatenate(blocks, axis=0)
+        top = tall.astype(BF16)
+        low = (tall - top.astype(F32)).astype(BF16)
+        got = dot(jnp.concatenate([top, low], axis=0), place)
+        return got[: tall.shape[0]] + got[tall.shape[0] :]
+
+    place_src, place_dst = iota((4 * half, inner), 0), iota((4 * half, inner), 1)
+    place = place_dst == 4 * (place_src % side_cells - HALO) + place_src // half
+    place = place.astype(F32).astype(BF16)
+    blocks = []
+    for c in range(3):
+        for h in range(2):
+            mine = [own[h, q] * inverse[q, 0:4, h * half : (h + 1) * half] for q in range(4)]
+            blocks.append(jnp.concatenate([spread_rows(p, c, keep[h]) for p in mine], axis=1))
+    mine = placed(blocks, place)
+
+    slot = place_src % side_cells
+    from_left = place_dst == 4 * (slot % HALO) + slot // HALO
+    from_right = place_dst == 4 * (tile - HALO + slot % HALO) + slot // HALO
+    pair_q = 2 * (place_src // half - 2) + place_src % half // (half // 2)
+    from_pair = place_dst == 4 * (slot - HALO) + pair_q
+    part = place_src // half
+    rim_place = jnp.where(
+        part == 0, from_left.astype(F32), jnp.where(part == 1, from_right.astype(F32), from_pair.astype(F32))
+    ).astype(BF16)
+    scales = []
+    for h in range(2):
+        here = [inverse[q, 0:4, h * half : (h + 1) * half] for q in range(4)]
+        sides = []
+        for rim in (HALO, tile):
+            dense = pltpu.roll(here[0], (half - rim) % half, 1)
+            for q in range(1, 4):
+                turned = pltpu.roll(here[q], (HALO * q - rim) % half, 1)
+                dense = jnp.where(where_b // HALO == q, turned, dense)
+            sides.append(dense)
+        for pair in range(2):
+            even, odd = here[2 * pair], here[2 * pair + 1]
+            if h == 0:
+                even = pltpu.roll(even, half // 2, 1)
+            else:
+                odd = pltpu.roll(odd, half // 2, 1)
+            sides.append(jnp.where(lower_half, even, odd))
+        scales.append(sides)
 
     for_all(lambda n, m: batch(rims, m, send2, recv2).wait_recv())
 
-    blocks = [[], [], []]
-    for h in range(2):
-        pieces = []
-        lft = rims[h] + rims[4 + h]
-        rgt = rims[2 + h] + rims[6 + h]
-        for q in range(4):
-            beyond = rims[8 + 2 * h + q // 2]
-            if (q + h) % 2 == 0:
-                beyond = pltpu.roll(beyond, half // 2, 1)
-            lft_q = pltpu.roll(lft, (HALO - HALO * q) % half, 1)
-            rgt_q = pltpu.roll(rgt, (tile - HALO * q) % half, 1)
-            mid = own[h, q] + beyond + jnp.where(where_b < side_cells // 2, lft_q, rgt_q)
-            pieces.append(mid * inverse[q][:, h * half : (h + 1) * half])
-        for c in range(3):
-            spread_rows = [
-                jnp.where(keep[h], jnp.broadcast_to(p[c : c + 1], (8, half)), 0.0) for p in pieces
+    blocks = []
+    for c in range(3):
+        for h in range(2):
+            got = [
+                (rims[h] + rims[4 + h]) * scales[h][0],
+                (rims[2 + h] + rims[6 + h]) * scales[h][1],
+                rims[8 + 2 * h] * scales[h][2],
+                rims[9 + 2 * h] * scales[h][3],
             ]
-            blocks[c].append(jnp.concatenate(spread_rows, axis=1))
-    tall = jnp.concatenate([b for c in range(3) for b in blocks[c]], axis=0)
-    top = tall.astype(BF16)
-    low = (tall - top.astype(F32)).astype(BF16)
-    image = dot(top, place) + dot(low, place)
-    out[...] = image.reshape(3, inner, inner)
+            masks = [keep[h], keep[h], beyond_row[h], beyond_row[h]]
+            blocks.append(
+                jnp.concatenate([spread_rows(p, c, m) for p, m in zip(got, masks)], axis=1)
+            )
+    out[...] = (mine + placed(blocks, rim_place)).reshape(3, inner, inner)
 
     for_all(lambda n, m: batch(cells, n, send1, recv1).wait_send())
     for_all(lambda n, m: batch(rims, m, send2, recv2).wait_send())
@@ -494,6 +544,11 @@
                 pltpu.SMEM(lim_c.shape, jnp.int32),
                 pltpu.VMEM((9, 8, w_in.shape[2]), F32),
                 pltpu.VMEM((9, 8, w_out.shape[2]), F32),
+                pltpu.VMEM((384, w_in.shape[2]), BF16),
+                pltpu.VMEM((w_mid.shape[2], 9 * w_mid.shape[1]), BF16),
+                pltpu.VMEM((w_low.shape[2], 9 * w_low.shape[1]), BF16),
+                pltpu.VMEM((4, 8, 2 * half), F32),
+                pltpu.VMEM((4, 8, 2 * half), F32),
                 pltpu.VMEM((2, 4, 4, half), F32),
                 pltpu.VMEM((2, 2, 4, half), F32),
                 pltpu.VMEM((2, 2, 4, half), F32),

time: 13.7 us -> 12.9 us (0.942)
  Pallas kernels: 13 us -> 12.1 us
    pallas_call x1, Pallas kernels: 13 us -> 12.1 us  [per_device(): pl.pallas_call(functools.partial(kernel, nr, nc), out_shape=pltpu.VMEM((w...]
where the time goes in v3:
time: 12.9 us; the launch traced here: 12.7 us
  Pallas kernels  12.1 us (94%)
  local copies, waits for them, and re-layouts  0.61 us (5%)
    pallas_call x1, Pallas kernels, per_device(): pl.pallas_call(functools.partial(kernel, nr, nc), out_shape=pltpu.VMEM((w...  12.1 us
    unnamed x1, local copies, waits for them, and re-layouts  0.61 us

profile of v3, /device:TPU:1, one launch (start us, length us, event | category | flops | bytes accessed | tf_op | source)
XLA Modules:
  0.0 12.7 jit_solution(3750480800352785576)
XLA Ops:
  0.0 12.1 %decode.1 = f32[3,16,16]{2,1,0:T(8,128)S(1)} custom-call(bf16[4,4,4]{2,1,0:T(4,128)(2,1)} %lat.1, bf16[9,4,512]{2,1,0:T(4,128)(2,1)} %w_in.1, bf16[9,256,512]{2,1,0:T(8,128)(2,1)} %w_mid.1, bf16[9,128,256]{2,1,0:T(8,128)(2,1)} %w_low.1, bf16[9,3,128]{2,1,0:T(4,128)(2,1)} %w_out.1, s32[4,32]{1,0:T(4,128)} %ramp_r.1, s32[4,32]{1,0:T(4,128)} %ramp_c.1, ...), custom_call_target="tpu_custom_call" | custom-call | tf_op jit(solution)/shard_map/decode/pallas_call | solution.py:530
  12.1 0.6 %copy.11 = f32[3,16,16]{2,1,0:T(8,128)} copy(f32[3,16,16]{2,1,0:T(8,128)S(1)} %decode.1) | data formatting | bytes 6144

commit v4 on v3

--- a/solution.py
+++ b/solution.py
@@ -134,9 +134,9 @@
 
 def kernel(
     nr, nc, lat, w_in, w_mid, w_low, w_out, ramp_r, ramp_c, lim_r, lim_c, out,
-    cells, wi, wm, wl, wo, tr, tc, lr, lc, wi32, wo32, wc, wmt, wlt,
+    cells, wi, wm, wl, wo, tables, limits, wi32, wo32, wc, wmt, wlt,
     blend, inverse, own, side_out, vert_out, rims,
-    local_sem, ready, send1, recv1, send2, recv2,
+    local_sem, ready, recv1, recv2,
 ):
     row, col = lax.axis_index("rows"), lax.axis_index("cols")
 
@@ -153,27 +153,35 @@
 
     loads = [
         pltpu.make_async_copy(src, dst, local_sem.at[k])
-        for k, (src, dst) in enumerate(
-            [
-                (lat, cells.at[4]),
-                (w_in, wi),
-                (ramp_r, tr),
-                (ramp_c, tc),
-                (lim_r, lr),
-                (lim_c, lc),
-                (w_out, wo),
-                (w_mid, wm),
-                (w_low, wl),
-            ]
-        )
+        for k, src, dst in [
+            (0, lat, cells.at[4]),
+            (1, w_in, wi),
+            (2, ramp_r, tables.at[0]),
+            (2, ramp_c, tables.at[1]),
+            (3, lim_r, limits.at[0]),
+            (3, lim_c, limits.at[1]),
+            (4, w_mid, wm),
+            (5, w_low, wl),
+        ]
     ]
+    load_out = pltpu.make_async_copy(w_out, wo, local_sem.at[1])
+    send1, send2 = local_sem.at[0], local_sem.at[0]
     for load in loads:
         load.start()
 
+    def mutual(dr, dc):
+        return jnp.logical_and(row == (0 if dr > 0 else 1), col % 2 == (1 if dc > 0 else 0))
+
+    def one_way(dr, dc):
+        there = exists(dr, dc)
+        return jnp.logical_and(there, jnp.logical_not(mutual(dr, dc))) if dr * dc else there
+
     barrier = pltpu.get_barrier_semaphore()
-    for k, dr, dc in LATER:
-
-        @pl.when(exists(dr, dc))
+    greeted = [(exists(dr, dc), dr, dc) for _, dr, dc in LATER]
+    greeted += [(jnp.logical_and(exists(-1, dc), mutual(-1, dc)), -1, dc) for dc in (-1, 1)]
+    for there, dr, dc in greeted:
+
+        @pl.when(there)
         def _():
             pl.semaphore_signal(barrier, inc=1, device_id=device(dr, dc), device_id_type=MESH)
 
@@ -246,6 +254,9 @@
     earlier = (col > 0).astype(jnp.int32) + (row > 0).astype(jnp.int32) * (
         1 + (col > 0).astype(jnp.int32) + (col < nc - 1).astype(jnp.int32)
     )
+    if nr > 1:
+        for dc in (-1, 1):
+            earlier += jnp.logical_and(exists(1, dc), mutual(1, dc)).astype(jnp.int32)
 
     @pl.when(row + col > 0)
     def _():
@@ -253,7 +264,7 @@
 
     for k, dr, dc in EARLIER:
 
-        @pl.when(exists(dr, dc))
+        @pl.when(one_way(dr, dc))
         def _():
             pl.semaphore_signal(
                 ready.at[3 - k], inc=1, device_id=device(dr, dc), device_id_type=MESH
@@ -266,10 +277,17 @@
         def _():
             copies(k, dr, dc)[0].start()
 
+    for k, dr, dc in LATER:
+        if dr * dc:
+
+            @pl.when(jnp.logical_and(exists(dr, dc), mutual(dr, dc)))
+            def _():
+                copies(k, dr, dc)[0].start()
+
     def send_later(entries):
         for k, dr, dc in entries:
 
-            @pl.when(exists(dr, dc))
+            @pl.when(one_way(dr, dc))
             def _():
                 pl.semaphore_wait(ready.at[k - 4], 1)
                 copies(k, dr, dc)[0].start()
@@ -286,6 +304,7 @@
     wide = chans * side_cells
 
     loads[1].wait()
+    load_out.start()
     wi32[...] = jnp.zeros(wi32.shape, F32)
     wi32[:, 0 : wi.shape[1], :] = wi[...].astype(F32)
     wi72 = wi32[...].reshape(72, wi32.shape[2]).astype(BF16)
@@ -296,8 +315,8 @@
         & (src % 128 < 3 * wide)
     )
     wc[...] = dot(pick.astype(F32).astype(BF16), wi72).astype(BF16)
-    for k in (2, 3, 4, 5):
-        loads[k].wait()
+    pltpu.make_async_copy(tables, tables, local_sem.at[2]).wait()
+    pltpu.make_async_copy(limits, limits, local_sem.at[3]).wait()
 
     spread_r = (iota((size, span), 1) // side_cells == iota((size, span), 0)).astype(F32)
     spread_c = [
@@ -305,8 +324,8 @@
         for q in range(4)
     ]
     spread_c = jnp.concatenate(spread_c, axis=1)
-    row_w = dot(table_rows(tr[...].astype(F32), lr, row, nr, margin, inner), spread_r.astype(BF16))
-    col_w = dot(table_rows(tc[...].astype(F32), lc, col, nc, margin, inner), spread_c.astype(BF16))
+    row_w = dot(table_rows(tables[0].astype(F32), limits.at[0], row, nr, margin, inner), spread_r.astype(BF16))
+    col_w = dot(table_rows(tables[1].astype(F32), limits.at[1], col, nc, margin, inner), spread_c.astype(BF16))
     lane = iota((1, span), 1)
     r_of, b_of = lane // side_cells, lane % side_cells
     inside = (
@@ -321,18 +340,19 @@
 
     send_later([e for e in LATER if e[1] != 0])
 
-    loads[6].wait()
+    load_out.wait()
     wo32[...] = jnp.zeros(wo32.shape, F32)
     wo32[:, 0 : wo.shape[1], :] = wo[...].astype(F32)
-    loads[7].wait()
+    loads[6].wait()
     out_mid = wm.shape[1]
     for t in range(9):
         wmt[:, out_mid * t : out_mid * (t + 1)] = wm[t].T
-    loads[8].wait()
+    loads[7].wait()
     out_low = wl.shape[1]
     for t in range(9):
         wlt[:, out_low * t : out_low * (t + 1)] = wl[t].T
 
+    for_all(lambda n, m: batch(cells, n, send1, recv1).wait_send())
     for_all(lambda n, m: batch(cells, n, send1, recv1).wait_recv())
 
     cell = [cells[k].astype(F32) for k in range(9)]
@@ -429,6 +449,16 @@
                 turned = pltpu.roll(own[h, q], (HALO * q - rim) % half, 1)
                 dense = jnp.where(where_b // HALO == q, turned, dense)
             side_out[k, h] = dense
+
+    def send_rims(entries):
+        for k, (dr, dc) in entries:
+
+            @pl.when(exists(dr, dc))
+            def _():
+                copies(k, dr, dc)[1].start()
+
+    send_rims([e for e in FAR_FIRST if e[1][1] != 0])
+    for h in range(2):
         for pair in range(2):
             even, odd = own[h, 2 * pair], own[h, 2 * pair + 1]
             if h == 0:
@@ -436,12 +466,7 @@
             else:
                 even = pltpu.roll(even, half // 2, 1)
             vert_out[h, pair] = jnp.where(lower_half, even, odd)
-
-    for k, (dr, dc) in FAR_FIRST:
-
-        @pl.when(exists(dr, dc))
-        def _():
-            copies(k, dr, dc)[1].start()
+    send_rims([e for e in FAR_FIRST if e[1][1] == 0])
 
     lane_row = iota((8, half), 1) // side_cells
     sublane = iota((8, half), 0)
@@ -513,7 +538,6 @@
             )
     out[...] = (mine + placed(blocks, rim_place)).reshape(3, inner, inner)
 
-    for_all(lambda n, m: batch(cells, n, send1, recv1).wait_send())
     for_all(lambda n, m: batch(rims, m, send2, recv2).wait_send())
 
 
@@ -538,10 +562,8 @@
                 pltpu.VMEM(w_mid.shape, BF16),
                 pltpu.VMEM(w_low.shape, BF16),
                 pltpu.VMEM(w_out.shape, BF16),
-                pltpu.VMEM(ramp_r.shape, jnp.int32),
-                pltpu.VMEM(ramp_c.shape, jnp.int32),
-                pltpu.SMEM(lim_r.shape, jnp.int32),
-                pltpu.SMEM(lim_c.shape, jnp.int32),
+                pltpu.VMEM((2,) + ramp_r.shape, jnp.int32),
+                pltpu.SMEM((2,) + lim_r.shape, jnp.int32),
                 pltpu.VMEM((9, 8, w_in.shape[2]), F32),
                 pltpu.VMEM((9, 8, w_out.shape[2]), F32),
                 pltpu.VMEM((384, w_in.shape[2]), BF16),
@@ -553,10 +575,8 @@
                 pltpu.VMEM((2, 2, 4, half), F32),
                 pltpu.VMEM((2, 2, 4, half), F32),
                 pltpu.VMEM((12, 4, half), F32),
-                dma((9,)),
+                dma((6,)),
                 pltpu.SemaphoreType.REGULAR((4,)),
-                dma,
-                dma,
                 dma,
                 dma,
             ],

time: 12.9 us -> 13.2 us (1.023)
  the two profiles are of different devices: /device:TPU:1 before, /device:TPU:0 now
where the time goes in v4:
time: 13.2 us; the launch traced here: 13 us
  Pallas kernels  12.4 us (94%)
  local copies, waits for them, and re-layouts  0.61 us (5%)
    pallas_call x1, Pallas kernels, per_device(): pl.pallas_call(functools.partial(kernel, nr, nc), out_shape=pltpu.VMEM((w...  12.4 us
    unnamed x1, local copies, waits for them, and re-layouts  0.61 us

profile of v4, /device:TPU:0, one launch (start us, length us, event | category | flops | bytes accessed | tf_op | source)
XLA Modules:
  0.0 13.0 jit_solution(15877459877983053618)
XLA Ops:
  0.0 12.4 %decode.1 = f32[3,16,16]{2,1,0:T(8,128)S(1)} custom-call(bf16[4,4,4]{2,1,0:T(4,128)(2,1)} %lat.1, bf16[9,4,512]{2,1,0:T(4,128)(2,1)} %w_in.1, bf16[9,256,512]{2,1,0:T(8,128)(2,1)} %w_mid.1, bf16[9,128,256]{2,1,0:T(8,128)(2,1)} %w_low.1, bf16[9,3,128]{2,1,0:T(4,128)(2,1)} %w_out.1, s32[4,32]{1,0:T(4,128)} %ramp_r.1, s32[4,32]{1,0:T(4,128)} %ramp_c.1, ...), custom_call_target="tpu_custom_call" | custom-call | tf_op jit(solution)/shard_map/decode/pallas_call | solution.py:554
  12.4 0.6 %copy.11 = f32[3,16,16]{2,1,0:T(8,128)} copy(f32[3,16,16]{2,1,0:T(8,128)S(1)} %decode.1) | data formatting | bytes 6144

commit v5 on v4

--- a/solution.py
+++ b/solution.py
@@ -14,8 +14,7 @@
 BF16 = jnp.bfloat16
 AROUND = [(dr, dc) for dr in (-1, 0, 1) for dc in (-1, 0, 1) if (dr, dc) != (0, 0)]
 FAR_FIRST = sorted(enumerate(AROUND), key=lambda e: -abs(e[1][0]) - abs(e[1][1]))
-EARLIER = [(k, *to) for k, to in FAR_FIRST if k < 4]
-LATER = [(k, *AROUND[k]) for k in range(4, 8)]
+READY = {k: n for n, k in enumerate((3, 4, 5, 6, 7))}
 
 
 def iota(shape, dim):
@@ -169,21 +168,44 @@
     for load in loads:
         load.start()
 
+    odd = col % 2 == 1
+
     def mutual(dr, dc):
-        return jnp.logical_and(row == (0 if dr > 0 else 1), col % 2 == (1 if dc > 0 else 0))
-
-    def one_way(dr, dc):
+        return jnp.logical_and(row == (0 if dr > 0 else 1), odd if dc > 0 else jnp.logical_not(odd))
+
+    def leads(dr, dc):
         there = exists(dr, dc)
-        return jnp.logical_and(there, jnp.logical_not(mutual(dr, dc))) if dr * dc else there
+        return there if dr > 0 else jnp.logical_and(there, odd)
+
+    def greets(dr, dc):
+        there = exists(dr, dc)
+        if dr < 0:
+            return jnp.logical_and(there, mutual(dr, dc)) if dc else None
+        return leads(dr, dc)
+
+    def greeted_by(dr, dc):
+        there = exists(dr, dc)
+        if dr > 0:
+            return jnp.logical_and(there, mutual(dr, dc)) if dc else None
+        return there if dr < 0 else jnp.logical_and(there, jnp.logical_not(odd))
+
+    def alone(test, other):
+        return test if other is None else jnp.logical_and(test, jnp.logical_not(other))
 
     barrier = pltpu.get_barrier_semaphore()
-    greeted = [(exists(dr, dc), dr, dc) for _, dr, dc in LATER]
-    greeted += [(jnp.logical_and(exists(-1, dc), mutual(-1, dc)), -1, dc) for dc in (-1, 1)]
-    for there, dr, dc in greeted:
-
-        @pl.when(there)
-        def _():
-            pl.semaphore_signal(barrier, inc=1, device_id=device(dr, dc), device_id_type=MESH)
+    earlier = 0
+    for dr, dc in AROUND:
+        test = greets(dr, dc)
+        if test is not None:
+
+            @pl.when(test)
+            def _():
+                pl.semaphore_signal(barrier, inc=1, device_id=device(dr, dc), device_id_type=MESH)
+
+    for dr, dc in AROUND:
+        test = greeted_by(dr, dc)
+        if test is not None:
+            earlier += test.astype(jnp.int32)
 
     def slot_of(dr, dc):
         up_down, left_right = (dr + 1) // 2, (dc + 1) // 2
@@ -251,48 +273,38 @@
             pixels = slot_of(dr, dc)
             pixels[...] = jnp.zeros(pixels.shape, F32)
 
-    earlier = (col > 0).astype(jnp.int32) + (row > 0).astype(jnp.int32) * (
-        1 + (col > 0).astype(jnp.int32) + (col < nc - 1).astype(jnp.int32)
-    )
-    if nr > 1:
-        for dc in (-1, 1):
-            earlier += jnp.logical_and(exists(1, dc), mutual(1, dc)).astype(jnp.int32)
-
-    @pl.when(row + col > 0)
+    @pl.when(earlier > 0)
     def _():
         pl.semaphore_wait(barrier, earlier)
 
-    for k, dr, dc in EARLIER:
-
-        @pl.when(one_way(dr, dc))
-        def _():
-            pl.semaphore_signal(
-                ready.at[3 - k], inc=1, device_id=device(dr, dc), device_id_type=MESH
-            )
+    for k, (dr, dc) in FAR_FIRST:
+        if dr <= 0:
+            by = greeted_by(dr, dc)
+
+            @pl.when(alone(by, greets(dr, dc) if dr * dc else None))
+            def _():
+                pl.semaphore_signal(
+                    ready.at[READY[7 - k]], inc=1, device_id=device(dr, dc), device_id_type=MESH
+                )
 
     loads[0].wait()
-    for k, dr, dc in EARLIER:
-
-        @pl.when(exists(dr, dc))
-        def _():
-            copies(k, dr, dc)[0].start()
-
-    for k, dr, dc in LATER:
-        if dr * dc:
-
-            @pl.when(jnp.logical_and(exists(dr, dc), mutual(dr, dc)))
+    for k, (dr, dc) in FAR_FIRST:
+        by = greeted_by(dr, dc)
+        if by is not None:
+
+            @pl.when(by)
             def _():
                 copies(k, dr, dc)[0].start()
 
     def send_later(entries):
-        for k, dr, dc in entries:
-
-            @pl.when(one_way(dr, dc))
+        for k, (dr, dc) in entries:
+
+            @pl.when(alone(leads(dr, dc), greeted_by(dr, dc) if dr else None))
             def _():
-                pl.semaphore_wait(ready.at[k - 4], 1)
+                pl.semaphore_wait(ready.at[READY[k]], 1)
                 copies(k, dr, dc)[0].start()
 
-    send_later([e for e in LATER if e[1] == 0])
+    send_later([e for e in enumerate(AROUND) if e[1][0] == 0])
 
     tile = lat.shape[1]
     side_cells = tile + 2 * HALO
@@ -338,7 +350,7 @@
             1.0 / jnp.where(inside, row_w[1:2] * cw[1:2], 1.0), (8, span)
         )
 
-    send_later([e for e in LATER if e[1] != 0])
+    send_later([e for e in enumerate(AROUND) if e[1][0] > 0])
 
     load_out.wait()
     wo32[...] = jnp.zeros(wo32.shape, F32)
@@ -449,24 +461,19 @@
                 turned = pltpu.roll(own[h, q], (HALO * q - rim) % half, 1)
                 dense = jnp.where(where_b // HALO == q, turned, dense)
             side_out[k, h] = dense
-
-    def send_rims(entries):
-        for k, (dr, dc) in entries:
-
-            @pl.when(exists(dr, dc))
-            def _():
-                copies(k, dr, dc)[1].start()
-
-    send_rims([e for e in FAR_FIRST if e[1][1] != 0])
-    for h in range(2):
         for pair in range(2):
-            even, odd = own[h, 2 * pair], own[h, 2 * pair + 1]
+            even, odds = own[h, 2 * pair], own[h, 2 * pair + 1]
             if h == 0:
-                odd = pltpu.roll(odd, half // 2, 1)
+                odds = pltpu.roll(odds, half // 2, 1)
             else:
                 even = pltpu.roll(even, half // 2, 1)
-            vert_out[h, pair] = jnp.where(lower_half, even, odd)
-    send_rims([e for e in FAR_FIRST if e[1][1] == 0])
+            vert_out[h, pair] = jnp.where(lower_half, even, odds)
+
+    for k, (dr, dc) in FAR_FIRST:
+
+        @pl.when(exists(dr, dc))
+        def _():
+            copies(k, dr, dc)[1].start()
 
     lane_row = iota((8, half), 1) // side_cells
     sublane = iota((8, half), 0)
@@ -513,12 +520,12 @@
                 dense = jnp.where(where_b // HALO == q, turned, dense)
             sides.append(dense)
         for pair in range(2):
-            even, odd = here[2 * pair], here[2 * pair + 1]
+            even, odds = here[2 * pair], here[2 * pair + 1]
             if h == 0:
                 even = pltpu.roll(even, half // 2, 1)
             else:
-                odd = pltpu.roll(odd, half // 2, 1)
-            sides.append(jnp.where(lower_half, even, odd))
+                odds = pltpu.roll(odds, half // 2, 1)
+            sides.append(jnp.where(lower_half, even, odds))
         scales.append(sides)
 
     for_all(lambda n, m: batch(rims, m, send2, recv2).wait_recv())
@@ -576,7 +583,7 @@
                 pltpu.VMEM((2, 2, 4, half), F32),
                 pltpu.VMEM((12, 4, half), F32),
                 dma((6,)),
-                pltpu.SemaphoreType.REGULAR((4,)),
+                pltpu.SemaphoreType.REGULAR((5,)),
                 dma,
                 dma,
             ],

time: 13.2 us -> 12.4 us (0.939)
  Pallas kernels: 12.4 us -> 11.7 us
    pallas_call x1, Pallas kernels: 12.4 us -> 11.7 us  [per_device(): pl.pallas_call(functools.partial(kernel, nr, nc), out_shape=pltpu.VMEM((w...]
where the time goes in v5:
time: 12.4 us; the launch traced here: 12.3 us
  Pallas kernels  11.7 us (94%)
  local copies, waits for them, and re-layouts  0.61 us (5%)
    pallas_call x1, Pallas kernels, per_device(): pl.pallas_call(functools.partial(kernel, nr, nc), out_shape=pltpu.VMEM((w...  11.7 us
    unnamed x1, local copies, waits for them, and re-layouts  0.61 us

profile of v5, /device:TPU:0, one launch (start us, length us, event | category | flops | bytes accessed | tf_op | source)
XLA Modules:
  0.0 12.3 jit_solution(7170231043966422431)
XLA Ops:
  0.0 11.7 %decode.1 = f32[3,16,16]{2,1,0:T(8,128)S(1)} custom-call(bf16[4,4,4]{2,1,0:T(4,128)(2,1)} %lat.1, bf16[9,4,512]{2,1,0:T(4,128)(2,1)} %w_in.1, bf16[9,256,512]{2,1,0:T(8,128)(2,1)} %w_mid.1, bf16[9,128,256]{2,1,0:T(8,128)(2,1)} %w_low.1, bf16[9,3,128]{2,1,0:T(4,128)(2,1)} %w_out.1, s32[4,32]{1,0:T(4,128)} %ramp_r.1, s32[4,32]{1,0:T(4,128)} %ramp_c.1, ...), custom_call_target="tpu_custom_call" | custom-call | tf_op jit(solution)/shard_map/decode/pallas_call | solution.py:561
  11.7 0.6 %copy.11 = f32[3,16,16]{2,1,0:T(8,128)} copy(f32[3,16,16]{2,1,0:T(8,128)S(1)} %decode.1) | data formatting | bytes 6144

commit v6 on v5

--- a/solution.py
+++ b/solution.py
@@ -164,7 +164,7 @@
         ]
     ]
     load_out = pltpu.make_async_copy(w_out, wo, local_sem.at[1])
-    send1, send2 = local_sem.at[0], local_sem.at[0]
+    send1, send2 = local_sem.at[0], local_sem.at[1]
     for load in loads:
         load.start()
 
@@ -296,14 +296,18 @@
             def _():
                 copies(k, dr, dc)[0].start()
 
-    def send_later(entries):
+    def send_later(entries, when=None):
         for k, (dr, dc) in entries:
-
-            @pl.when(alone(leads(dr, dc), greeted_by(dr, dc) if dr else None))
+            test = alone(leads(dr, dc), greeted_by(dr, dc) if dr else None)
+
+            @pl.when(test if when is None else jnp.logical_and(test, when))
             def _():
                 pl.semaphore_wait(ready.at[READY[k]], 1)
                 copies(k, dr, dc)[0].start()
 
+    below = [e for e in enumerate(AROUND) if e[1][0] > 0]
+    hurry = jnp.logical_or(greeted_by(1, -1), greeted_by(1, 1))
+    send_later(below, hurry)
     send_later([e for e in enumerate(AROUND) if e[1][0] == 0])
 
     tile = lat.shape[1]
@@ -350,7 +354,7 @@
             1.0 / jnp.where(inside, row_w[1:2] * cw[1:2], 1.0), (8, span)
         )
 
-    send_later([e for e in enumerate(AROUND) if e[1][0] > 0])
+    send_later(below, jnp.logical_not(hurry))
 
     load_out.wait()
     wo32[...] = jnp.zeros(wo32.shape, F32)
@@ -364,7 +368,6 @@
     for t in range(9):
         wlt[:, out_low * t : out_low * (t + 1)] = wl[t].T
 
-    for_all(lambda n, m: batch(cells, n, send1, recv1).wait_send())
     for_all(lambda n, m: batch(cells, n, send1, recv1).wait_recv())
 
     cell = [cells[k].astype(F32) for k in range(9)]
@@ -528,6 +531,7 @@
             sides.append(jnp.where(lower_half, even, odds))
         scales.append(sides)
 
+    for_all(lambda n, m: batch(cells, n, send1, recv1).wait_send())
     for_all(lambda n, m: batch(rims, m, send2, recv2).wait_recv())
 
     blocks = []

time: 12.4 us -> 12.2 us (0.984)
  the two profiles are of different devices: /device:TPU:0 before, /device:TPU:1 now
where the time goes in v6:
time: 12.2 us; the launch traced here: 12 us
  Pallas kernels  11.4 us (93%)
  local copies, waits for them, and re-layouts  0.61 us (5%)
    pallas_call x1, Pallas kernels, per_device(): pl.pallas_call(functools.partial(kernel, nr, nc), out_shape=pltpu.VMEM((w...  11.4 us
    unnamed x1, local copies, waits for them, and re-layouts  0.61 us

profile of v6, /device:TPU:1, one launch (start us, length us, event | category | flops | bytes accessed | tf_op | source)
XLA Modules:
  0.0 12.0 jit_solution(9053511945783002422)
XLA Ops:
  0.0 11.4 %decode.1 = f32[3,16,16]{2,1,0:T(8,128)S(1)} custom-call(bf16[4,4,4]{2,1,0:T(4,128)(2,1)} %lat.1, bf16[9,4,512]{2,1,0:T(4,128)(2,1)} %w_in.1, bf16[9,256,512]{2,1,0:T(8,128)(2,1)} %w_mid.1, bf16[9,128,256]{2,1,0:T(8,128)(2,1)} %w_low.1, bf16[9,3,128]{2,1,0:T(4,128)(2,1)} %w_out.1, s32[4,32]{1,0:T(4,128)} %ramp_r.1, s32[4,32]{1,0:T(4,128)} %ramp_c.1, ...), custom_call_target="tpu_custom_call" | custom-call | tf_op jit(solution)/shard_map/decode/pallas_call | solution.py:565
  11.4 0.6 %copy.11 = f32[3,16,16]{2,1,0:T(8,128)} copy(f32[3,16,16]{2,1,0:T(8,128)S(1)} %decode.1) | data formatting | bytes 6144

commit v7 on v6

--- a/solution.py
+++ b/solution.py
@@ -83,24 +83,29 @@
     ]
 
 
+def group_sum(x, width):
+    lane = iota(x.shape, 1) % width
+    parts = [x]
+    for k in range(1, width):
+        parts.append(jnp.where(lane >= k, pltpu.roll(x, k, 1), 0.0))
+        parts.append(jnp.where(lane < width - k, pltpu.roll(x, x.shape[1] - k, 1), 0.0))
+    while len(parts) > 1:
+        parts = [functools.reduce(jnp.add, parts[k : k + 2]) for k in range(0, len(parts), 2)]
+    return parts[0]
+
+
 def group_silu(phases):
     channels = phases[0].shape[-1]
     width = channels // NGROUPS
     count = channels // 128
     positions = len(phases) * phases[0].shape[0] * phases[0].shape[1]
     scale = 1.0 / (positions * width)
-    block = (iota((384, 128), 0) % 128 // width == iota((384, 128), 1) // width).astype(F32)
-    block = block.astype(BF16)
     total = jnp.sum(functools.reduce(jnp.add, phases), axis=(0, 1)).reshape(1, channels)
     squares = functools.reduce(jnp.add, [p * p for p in phases])
     squares = jnp.sum(squares, axis=(0, 1)).reshape(1, channels)
     rows = [x[:, k * 128 : (k + 1) * 128] for x in (total, squares) for k in range(count)]
     rows = jnp.concatenate(rows + [jnp.zeros((1, 128), F32)] * (8 - len(rows)), axis=0)
-    top = rows.astype(BF16)
-    rest = rows - top.astype(F32)
-    mid = rest.astype(BF16)
-    low = (rest - mid.astype(F32)).astype(BF16)
-    got = dot(jnp.concatenate([top, mid, low], axis=1), block) * scale
+    got = group_sum(rows, width) * scale
     center = got[:count]
     spread = jnp.maximum(got[count : 2 * count] - center * center, 0.0)
     factor = 0.5 * lax.rsqrt(spread + 1e-06)

time: 12.2 us -> 12.1 us (level)
    pallas_call x1, Pallas kernels: 11.4 us -> 11.3 us  [per_device(): pl.pallas_call(functools.partial(kernel, nr, nc), out_shape=pltpu.VMEM((w...]
where the time goes in v7:
time: 12.1 us; the launch traced here: 11.9 us
  Pallas kernels  11.3 us (93%)
  local copies, waits for them, and re-layouts  0.61 us (5%)
    pallas_call x1, Pallas kernels, per_device(): pl.pallas_call(functools.partial(kernel, nr, nc), out_shape=pltpu.VMEM((w...  11.3 us
    unnamed x1, local copies, waits for them, and re-layouts  0.61 us

profile of v7, /device:TPU:1, one launch (start us, length us, event | category | flops | bytes accessed | tf_op | source)
XLA Modules:
  0.0 11.9 jit_solution(16283414967393475091)
XLA Ops:
  0.0 11.3 %decode.1 = f32[3,16,16]{2,1,0:T(8,128)S(1)} custom-call(bf16[4,4,4]{2,1,0:T(4,128)(2,1)} %lat.1, bf16[9,4,512]{2,1,0:T(4,128)(2,1)} %w_in.1, bf16[9,256,512]{2,1,0:T(8,128)(2,1)} %w_mid.1, bf16[9,128,256]{2,1,0:T(8,128)(2,1)} %w_low.1, bf16[9,3,128]{2,1,0:T(4,128)(2,1)} %w_out.1, s32[4,32]{1,0:T(4,128)} %ramp_r.1, s32[4,32]{1,0:T(4,128)} %ramp_c.1, ...), custom_call_target="tpu_custom_call" | custom-call | tf_op jit(solution)/shard_map/decode/pallas_call | solution.py:570
  11.3 0.6 %copy.11 = f32[3,16,16]{2,1,0:T(8,128)} copy(f32[3,16,16]{2,1,0:T(8,128)S(1)} %decode.1) | data formatting | bytes 6144

commit v8 on v7

--- a/solution.py
+++ b/solution.py
@@ -14,6 +14,7 @@
 BF16 = jnp.bfloat16
 AROUND = [(dr, dc) for dr in (-1, 0, 1) for dc in (-1, 0, 1) if (dr, dc) != (0, 0)]
 FAR_FIRST = sorted(enumerate(AROUND), key=lambda e: -abs(e[1][0]) - abs(e[1][1]))
+BY_COLUMN = [3 * (t % 3) + t // 3 for t in range(9)]
 READY = {k: n for n, k in enumerate((3, 4, 5, 6, 7))}
 
 
@@ -139,7 +140,7 @@
 def kernel(
     nr, nc, lat, w_in, w_mid, w_low, w_out, ramp_r, ramp_c, lim_r, lim_c, out,
     cells, wi, wm, wl, wo, tables, limits, wi32, wo32, wc, wmt, wlt,
-    blend, inverse, own, side_out, vert_out, rims,
+    blend, inverse, places, scales, own, side_out, vert_out, rims,
     local_sem, ready, recv1, recv2,
 ):
     row, col = lax.axis_index("rows"), lax.axis_index("cols")
@@ -226,10 +227,15 @@
             return side_out.at[left_right]
         return vert_out.at[up_down] if dc == 0 else side_out.at[left_right, up_down]
 
+    def rows_of(slot, dr):
+        if dr == 0:
+            return cells.at[slot]
+        return cells.at[slot, :, pl.ds(0 if dr < 0 else lat.shape[1] - HALO, HALO)]
+
     def copies(k, dr, dc):
         first = pltpu.make_async_remote_copy(
-            src_ref=cells.at[4],
-            dst_ref=cells.at[(1 - dr) * 3 + 1 - dc],
+            src_ref=rows_of(4, dr),
+            dst_ref=rows_of((1 - dr) * 3 + 1 - dc, dr),
             send_sem=send1,
             recv_sem=recv1,
             device_id=device(dr, dc),
@@ -256,10 +262,10 @@
 
                 @pl.when(jnp.logical_and(above_below == v, beside == h))
                 def _():
-                    wait(v + h + v * h, 2 * (v + h) + v * h)
+                    wait(v + v * h + lat.shape[1] // HALO * h, 2 * (v + h) + v * h)
 
     def batch(ref, n, send, recv):
-        part = ref.at[pl.ds(0, n)]
+        part = ref.at[pl.ds(0, n), :, pl.ds(0, HALO)] if ref is cells else ref.at[pl.ds(0, n)]
         return pltpu.make_async_remote_copy(
             src_ref=part,
             dst_ref=part,
@@ -367,11 +373,44 @@
     loads[6].wait()
     out_mid = wm.shape[1]
     for t in range(9):
-        wmt[:, out_mid * t : out_mid * (t + 1)] = wm[t].T
+        wmt[:, out_mid * t : out_mid * (t + 1)] = wm[BY_COLUMN[t]].T
     loads[7].wait()
     out_low = wl.shape[1]
     for t in range(9):
-        wlt[:, out_low * t : out_low * (t + 1)] = wl[t].T
+        wlt[:, out_low * t : out_low * (t + 1)] = wl[BY_COLUMN[t]].T
+
+    where_b = iota((4, half), 1) % side_cells
+    lower_half = iota((4, half), 1) < half // 2
+    place_src, place_dst = iota((4 * half, inner), 0), iota((4 * half, inner), 1)
+    place = place_dst == 4 * (place_src % side_cells - HALO) + place_src // half
+    places[0] = place.astype(F32).astype(BF16)
+    slot = place_src % side_cells
+    from_left = place_dst == 4 * (slot % HALO) + slot // HALO
+    from_right = place_dst == 4 * (tile - HALO + slot % HALO) + slot // HALO
+    pair_q = 2 * (place_src // half - 2) + place_src % half // (half // 2)
+    from_pair = place_dst == 4 * (slot - HALO) + pair_q
+    part = place_src // half
+    places[1] = jnp.where(
+        part == 0, from_left.astype(F32), jnp.where(part == 1, from_right.astype(F32), from_pair.astype(F32))
+    ).astype(BF16)
+    for h in range(2):
+        here = [inverse[q, 0:4, h * half : (h + 1) * half] for q in range(4)]
+        sides = []
+        for rim in (HALO, tile):
+            dense = pltpu.roll(here[0], (half - rim) % half, 1)
+            for q in range(1, 4):
+                turned = pltpu.roll(here[q], (HALO * q - rim) % half, 1)
+                dense = jnp.where(where_b // HALO == q, turned, dense)
+            sides.append(dense)
+        for pair in range(2):
+            even, odds = here[2 * pair], here[2 * pair + 1]
+            if h == 0:
+                even = pltpu.roll(even, half // 2, 1)
+            else:
+                odds = pltpu.roll(odds, half // 2, 1)
+            sides.append(jnp.where(lower_half, even, odds))
+        for n, side in enumerate(sides):
+            scales[h, n] = side
 
     for_all(lambda n, m: batch(cells, n, send1, recv1).wait_recv())
 
@@ -399,7 +438,7 @@
     taps = dot(first, wmt[...])
     taps = [
         taps[:, out_mid * t : out_mid * (t + 1)].reshape(side_cells, side_cells, -1)
-        for t in range(9)
+        for t in BY_COLUMN
     ]
     second = conv_up([[taps]], 1)
     second = group_silu([second[py][px] for py in range(2) for px in range(2)])
@@ -408,7 +447,7 @@
 
     n = side_cells * side_cells
     products = dot(second, wlt[...])
-    products = [products[:, out_low * t : out_low * (t + 1)] for t in range(9)]
+    products = [products[:, out_low * t : out_low * (t + 1)] for t in BY_COLUMN]
     taps = [
         [
             [
@@ -431,8 +470,6 @@
     def tap(q, t):
         return colour[q][8 * t : 8 * t + 8]
 
-    where_b = iota((4, half), 1) % side_cells
-    lower_half = iota((4, half), 1) < half // 2
     sub_b = iota((8, span), 1) % side_cells
     sub_r = iota((8, span), 1) // side_cells
     row_ok = [sub_r > 0, None, sub_r < size - 1]
@@ -498,43 +535,12 @@
         got = dot(jnp.concatenate([top, low], axis=0), place)
         return got[: tall.shape[0]] + got[tall.shape[0] :]
 
-    place_src, place_dst = iota((4 * half, inner), 0), iota((4 * half, inner), 1)
-    place = place_dst == 4 * (place_src % side_cells - HALO) + place_src // half
-    place = place.astype(F32).astype(BF16)
     blocks = []
     for c in range(3):
         for h in range(2):
             mine = [own[h, q] * inverse[q, 0:4, h * half : (h + 1) * half] for q in range(4)]
             blocks.append(jnp.concatenate([spread_rows(p, c, keep[h]) for p in mine], axis=1))
-    mine = placed(blocks, place)
-
-    slot = place_src % side_cells
-    from_left = place_dst == 4 * (slot % HALO) + slot // HALO
-    from_right = place_dst == 4 * (tile - HALO + slot % HALO) + slot // HALO
-    pair_q = 2 * (place_src // half - 2) + place_src % half // (half // 2)
-    from_pair = place_dst == 4 * (slot - HALO) + pair_q
-    part = place_src // half
-    rim_place = jnp.where(
-        part == 0, from_left.astype(F32), jnp.where(part == 1, from_right.astype(F32), from_pair.astype(F32))
-    ).astype(BF16)
-    scales = []
-    for h in range(2):
-        here = [inverse[q, 0:4, h * half : (h + 1) * half] for q in range(4)]
-        sides = []
-        for rim in (HALO, tile):
-            dense = pltpu.roll(here[0], (half - rim) % half, 1)
-            for q in range(1, 4):
-                turned = pltpu.roll(here[q], (HALO * q - rim) % half, 1)
-                dense = jnp.where(where_b // HALO == q, turned, dense)
-            sides.append(dense)
-        for pair in range(2):
-            even, odds = here[2 * pair], here[2 * pair + 1]
-            if h == 0:
-                even = pltpu.roll(even, half // 2, 1)
-            else:
-                odds = pltpu.roll(odds, half // 2, 1)
-            sides.append(jnp.where(lower_half, even, odds))
-        scales.append(sides)
+    mine = placed(blocks, places[0])
 
     for_all(lambda n, m: batch(cells, n, send1, recv1).wait_send())
     for_all(lambda n, m: batch(rims, m, send2, recv2).wait_recv())
@@ -543,16 +549,16 @@
     for c in range(3):
         for h in range(2):
             got = [
-                (rims[h] + rims[4 + h]) * scales[h][0],
-                (rims[2 + h] + rims[6 + h]) * scales[h][1],
-                rims[8 + 2 * h] * scales[h][2],
-                rims[9 + 2 * h] * scales[h][3],
+                (rims[h] + rims[4 + h]) * scales[h, 0],
+                (rims[2 + h] + rims[6 + h]) * scales[h, 1],
+                rims[8 + 2 * h] * scales[h, 2],
+                rims[9 + 2 * h] * scales[h, 3],
             ]
             masks = [keep[h], keep[h], beyond_row[h], beyond_row[h]]
             blocks.append(
                 jnp.concatenate([spread_rows(p, c, m) for p, m in zip(got, masks)], axis=1)
             )
-    out[...] = (mine + placed(blocks, rim_place)).reshape(3, inner, inner)
+    out[...] = (mine + placed(blocks, places[1])).reshape(3, inner, inner)
 
     for_all(lambda n, m: batch(rims, m, send2, recv2).wait_send())
 
@@ -573,7 +579,7 @@
             in_specs=[anywhere] * 9,
             out_specs=pl.BlockSpec(memory_space=pltpu.VMEM),
             scratch_shapes=[
-                pltpu.VMEM((9,) + lat.shape, BF16),
+                pltpu.VMEM((max(9, 6 + 2 * (lat.shape[1] // HALO)),) + lat.shape, BF16),
                 pltpu.VMEM(w_in.shape, BF16),
                 pltpu.VMEM(w_mid.shape, BF16),
                 pltpu.VMEM(w_low.shape, BF16),
@@ -587,6 +593,8 @@
                 pltpu.VMEM((w_low.shape[2], 9 * w_low.shape[1]), BF16),
                 pltpu.VMEM((4, 8, 2 * half), F32),
                 pltpu.VMEM((4, 8, 2 * half), F32),
+                pltpu.VMEM((2, 4 * half, inner), BF16),
+                pltpu.VMEM((2, 4, 4, half), F32),
                 pltpu.VMEM((2, 4, 4, half), F32),
                 pltpu.VMEM((2, 2, 4, half), F32),
                 pltpu.VMEM((2, 2, 4, half), F32),

time: 12.1 us -> 12 us (level)
  no operation moved by 1% of the time
where the time goes in v8:
time: 12 us; the launch traced here: 11.9 us
  Pallas kernels  11.3 us (94%)
  local copies, waits for them, and re-layouts  0.61 us (5%)
    pallas_call x1, Pallas kernels, per_device(): pl.pallas_call(functools.partial(kernel, nr, nc), out_shape=pltpu.VMEM((w...  11.3 us
    unnamed x1, local copies, waits for them, and re-layouts  0.61 us

profile of v8, /device:TPU:1, one launch (start us, length us, event | category | flops | bytes accessed | tf_op | source)
XLA Modules:
  0.0 11.9 jit_solution(5543023127576621058)
XLA Ops:
  0.0 11.3 %decode.1 = f32[3,16,16]{2,1,0:T(8,128)S(1)} custom-call(bf16[4,4,4]{2,1,0:T(4,128)(2,1)} %lat.1, bf16[9,4,512]{2,1,0:T(4,128)(2,1)} %w_in.1, bf16[9,256,512]{2,1,0:T(8,128)(2,1)} %w_mid.1, bf16[9,128,256]{2,1,0:T(8,128)(2,1)} %w_low.1, bf16[9,3,128]{2,1,0:T(4,128)(2,1)} %w_out.1, s32[4,32]{1,0:T(4,128)} %ramp_r.1, s32[4,32]{1,0:T(4,128)} %ramp_c.1, ...), custom_call_target="tpu_custom_call" | custom-call | tf_op jit(solution)/shard_map/decode/pallas_call | solution.py:576
  11.3 0.6 %copy.11 = f32[3,16,16]{2,1,0:T(8,128)} copy(f32[3,16,16]{2,1,0:T(8,128)S(1)} %decode.1) | data formatting | bytes 6144

commit v9 on v8

--- a/solution.py
+++ b/solution.py
@@ -95,9 +95,8 @@
     return parts[0]
 
 
-def group_silu(phases):
+def group_silu(phases, width):
     channels = phases[0].shape[-1]
-    width = channels // NGROUPS
     count = channels // 128
     positions = len(phases) * phases[0].shape[0] * phases[0].shape[1]
     scale = 1.0 / (positions * width)
@@ -137,11 +136,11 @@
     return pair.astype(BF16)
 
 
-def kernel(
+def body(
     nr, nc, lat, w_in, w_mid, w_low, w_out, ramp_r, ramp_c, lim_r, lim_c, out,
     cells, wi, wm, wl, wo, tables, limits, wi32, wo32, wc, wmt, wlt,
     blend, inverse, places, scales, own, side_out, vert_out, rims,
-    local_sem, ready, recv1, recv2,
+    ready, recv1, recv2, local_sem,
 ):
     row, col = lax.axis_index("rows"), lax.axis_index("cols")
 
@@ -171,9 +170,6 @@
     ]
     load_out = pltpu.make_async_copy(w_out, wo, local_sem.at[1])
     send1, send2 = local_sem.at[0], local_sem.at[1]
-    for load in loads:
-        load.start()
-
     odd = col % 2 == 1
 
     def mutual(dr, dc):
@@ -200,14 +196,23 @@
 
     barrier = pltpu.get_barrier_semaphore()
     earlier = 0
-    for dr, dc in AROUND:
-        test = greets(dr, dc)
-        if test is not None:
-
-            @pl.when(test)
-            def _():
-                pl.semaphore_signal(barrier, inc=1, device_id=device(dr, dc), device_id_type=MESH)
-
+
+    def greet(entries):
+        for dr, dc in entries:
+            test = greets(dr, dc)
+            if test is not None:
+
+                @pl.when(test)
+                def _():
+                    pl.semaphore_signal(
+                        barrier, inc=1, device_id=device(dr, dc), device_id_type=MESH
+                    )
+
+    loads[0].start()
+    greet([e for e in AROUND if e[0] < 0])
+    for load in loads[1:]:
+        load.start()
+    greet([e for e in AROUND if e[0] >= 0])
     for dr, dc in AROUND:
         test = greeted_by(dr, dc)
         if test is not None:
@@ -373,7 +378,10 @@
     loads[6].wait()
     out_mid = wm.shape[1]
     for t in range(9):
-        wmt[:, out_mid * t : out_mid * (t + 1)] = wm[BY_COLUMN[t]].T
+        turned = wm[BY_COLUMN[t]].T
+        for n in range(out_mid // 128):
+            at = 128 * (9 * n + t)
+            wmt[:, at : at + 128] = turned[:, 128 * n : 128 * (n + 1)]
     loads[7].wait()
     out_low = wl.shape[1]
     for t in range(9):
@@ -432,16 +440,20 @@
     patches = [jnp.where(gap == dx - 1, spreaded, 0.0) for dx in range(3)]
     patches = jnp.concatenate(patches, axis=2).reshape(-1, 384).astype(BF16)
     first = dot(patches, wc[...]).reshape(side_cells, side_cells, -1)
-    (first,) = group_silu([first])
+    (first,) = group_silu([first], first.shape[2] // NGROUPS)
     first = first.reshape(side_cells * side_cells, -1).astype(BF16)
 
     taps = dot(first, wmt[...])
-    taps = [
-        taps[:, out_mid * t : out_mid * (t + 1)].reshape(side_cells, side_cells, -1)
-        for t in BY_COLUMN
-    ]
-    second = conv_up([[taps]], 1)
-    second = group_silu([second[py][px] for py in range(2) for px in range(2)])
+    chunks = []
+    for n in range(out_mid // 128):
+        part = [
+            taps[:, 128 * (9 * n + t) : 128 * (9 * n + t + 1)].reshape(side_cells, side_cells, -1)
+            for t in BY_COLUMN
+        ]
+        part = conv_up([[part]], 1)
+        part = [part[py][px] for py in range(2) for px in range(2)]
+        chunks.append(group_silu(part, out_mid // NGROUPS))
+    second = [jnp.concatenate(parts, axis=2) for parts in zip(*chunks)]
     second = jnp.concatenate(second, axis=0)
     second = second.reshape(-1, second.shape[2]).astype(BF16)
 
@@ -459,7 +471,8 @@
         for py in range(2)
     ]
     third = conv_up(taps, 2)
-    third = group_silu([third[qy][qx] for qy in range(4) for qx in range(4)])
+    third = [third[qy][qx] for qy in range(4) for qx in range(4)]
+    third = group_silu(third, out_low // NGROUPS)
 
     wo72 = wo32[...].reshape(72, wo32.shape[2]).astype(BF16)
     colour = []
@@ -561,6 +574,13 @@
     out[...] = (mine + placed(blocks, places[1])).reshape(3, inner, inner)
 
     for_all(lambda n, m: batch(rims, m, send2, recv2).wait_send())
+
+
+def kernel(nr, nc, *refs):
+    def scoped(local_sem):
+        body(nr, nc, *refs, local_sem)
+
+    pl.run_scoped(scoped, pltpu.SemaphoreType.DMA((6,)))
 
 
 def solution(mesh):
@@ -599,7 +619,6 @@
                 pltpu.VMEM((2, 2, 4, half), F32),
                 pltpu.VMEM((2, 2, 4, half), F32),
                 pltpu.VMEM((12, 4, half), F32),
-                dma((6,)),
                 pltpu.SemaphoreType.REGULAR((5,)),
                 dma,
                 dma,

time: 12 us -> 12 us (level)
  no operation moved by 1% of the time
where the time goes in v9:
time: 12 us; the launch traced here: 11.8 us
  Pallas kernels  11.2 us (93%)
  local copies, waits for them, and re-layouts  0.61 us (5%)
    pallas_call x1, Pallas kernels, per_device(): pl.pallas_call(functools.partial(kernel, nr, nc), out_shape=pltpu.VMEM((w...  11.2 us
    unnamed x1, local copies, waits for them, and re-layouts  0.61 us

profile of v9, /device:TPU:1, one launch (start us, length us, event | category | flops | bytes accessed | tf_op | source)
XLA Modules:
  0.0 11.8 jit_solution(3959653923724017816)
XLA Ops:
  0.0 11.2 %decode.1 = f32[3,16,16]{2,1,0:T(8,128)S(1)} custom-call(bf16[4,4,4]{2,1,0:T(4,128)(2,1)} %refs_0_.1, bf16[9,4,512]{2,1,0:T(4,128)(2,1)} %refs_1_.1, bf16[9,256,512]{2,1,0:T(8,128)(2,1)} %refs_2_.1, bf16[9,128,256]{2,1,0:T(8,128)(2,1)} %refs_3_.1, bf16[9,3,128]{2,1,0:T(4,128)(2,1)} %refs_4_.1, s32[4,32]{1,0:T(4,128)} %refs_5_.1, s32[4,32]{1,0:T(4,128)} %refs_6_.1, ...), custom_call_target="tpu_custom_call" | custom-call | tf_op jit(solution)/shard_map/decode/pallas_call | solution.py:596
  11.2 0.6 %copy.11 = f32[3,16,16]{2,1,0:T(8,128)} copy(f32[3,16,16]{2,1,0:T(8,128)S(1)} %decode.1) | data formatting | bytes 6144

commit v10 on v9

--- a/solution.py
+++ b/solution.py
@@ -95,7 +95,7 @@
     return parts[0]
 
 
-def group_silu(phases, width):
+def group_terms(phases, width):
     channels = phases[0].shape[-1]
     count = channels // 128
     positions = len(phases) * phases[0].shape[0] * phases[0].shape[1]
@@ -112,11 +112,17 @@
     offset = center * factor
     factor = jnp.concatenate([factor[k : k + 1] for k in range(count)], axis=1)[None]
     offset = jnp.concatenate([offset[k : k + 1] for k in range(count)], axis=1)[None]
-    result = []
-    for p in phases:
-        half = p * factor - offset
-        result.append(half + half * jnp.tanh(half))
-    return result
+    return factor, offset
+
+
+def silu(p, terms):
+    half = p * terms[0] - terms[1]
+    return half + half * jnp.tanh(half)
+
+
+def group_silu(phases, width):
+    terms = group_terms(phases, width)
+    return [silu(p, terms) for p in phases]
 
 
 def table_rows(table, limits, index, count, margin, inner):
@@ -139,7 +145,7 @@
 def body(
     nr, nc, lat, w_in, w_mid, w_low, w_out, ramp_r, ramp_c, lim_r, lim_c, out,
     cells, wi, wm, wl, wo, tables, limits, wi32, wo32, wc, wmt, wlt,
-    blend, inverse, places, scales, own, side_out, vert_out, rims,
+    blend, inverse, places, scales, own, up_out, side_out, vert_out, rims,
     ready, recv1, recv2, local_sem,
 ):
     row, col = lax.axis_index("rows"), lax.axis_index("cols")
@@ -230,7 +236,9 @@
         up_down, left_right = (dr + 1) // 2, (dc + 1) // 2
         if dr == 0:
             return side_out.at[left_right]
-        return vert_out.at[up_down] if dc == 0 else side_out.at[left_right, up_down]
+        if dc == 0:
+            return vert_out.at[up_down]
+        return up_out.at[left_right] if dr < 0 else side_out.at[left_right, 1]
 
     def rows_of(slot, dr):
         if dr == 0:
@@ -472,66 +480,101 @@
     ]
     third = conv_up(taps, 2)
     third = [third[qy][qx] for qy in range(4) for qx in range(4)]
-    third = group_silu(third, out_low // NGROUPS)
+    terms = group_terms(third, out_low // NGROUPS)
 
     wo72 = wo32[...].reshape(72, wo32.shape[2]).astype(BF16)
-    colour = []
-    for qx in range(4):
-        rows = jnp.stack([third[4 * qy + qx] for qy in range(4)], axis=1)
-        colour.append(nt_dot(wo72, rows.reshape(span, rows.shape[-1]).astype(BF16)))
-
-    def tap(q, t):
-        return colour[q][8 * t : 8 * t + 8]
-
-    sub_b = iota((8, span), 1) % side_cells
-    sub_r = iota((8, span), 1) // side_cells
-    row_ok = [sub_r > 0, None, sub_r < size - 1]
-    col_ok = [sub_b > 0, None, sub_b < side_cells - 1]
-
-    def moved(x, dy, dx):
-        shift = (side_cells * (1 - dy) + 1 - dx) % span
-        x = pltpu.roll(x, shift, 1) if shift else x
-        ok = [m for m in (row_ok[dy], col_ok[dx]) if m is not None]
-        return jnp.where(functools.reduce(jnp.logical_and, ok), x, 0.0) if ok else x
-
-    for q in range(4):
-        value = None
-        for dy in range(3):
-            near = tap(q, 3 * dy + 1)
-            if q > 0:
-                near = near + tap(q - 1, 3 * dy)
-            if q < 3:
-                near = near + tap(q + 1, 3 * dy + 2)
-            term = moved(near, dy, 1)
-            if q == 0:
-                term = term + moved(tap(3, 3 * dy), dy, 0)
-            if q == 3:
-                term = term + moved(tap(0, 3 * dy + 2), dy, 2)
-            value = term if value is None else value + term
-        value = value * blend[q]
-        for h in range(2):
-            own[h, q] = value[0:4, h * half : (h + 1) * half]
-
+    def colours(lo, hi):
+        got = []
+        for pair in range(2):
+            rows = [
+                jnp.stack([silu(third[4 * qy + qx][lo:hi], terms) for qy in range(4)], axis=1)
+                for qx in (2 * pair, 2 * pair + 1)
+            ]
+            rows = jnp.concatenate([r.reshape(-1, r.shape[-1]) for r in rows], axis=0)
+            both = nt_dot(wo72, rows.astype(BF16))
+            got += [both[:, :half], both[:, half:]]
+        return got
+
+    def blended(colour, at):
+        lanes = colour[0].shape[1]
+        sub_b = iota((8, lanes), 1) % side_cells
+        sub_r = iota((8, lanes), 1) // side_cells
+        row_ok = [sub_r > 0, None, sub_r < lanes // side_cells - 1]
+        col_ok = [sub_b > 0, None, sub_b < side_cells - 1]
+
+        def tap(q, t):
+            return colour[q][8 * t : 8 * t + 8]
+
+        def moved(x, dy, dx):
+            shift = (side_cells * (1 - dy) + 1 - dx) % lanes
+            x = pltpu.roll(x, shift, 1) if shift else x
+            ok = [m for m in (row_ok[dy], col_ok[dx]) if m is not None]
+            return jnp.where(functools.reduce(jnp.logical_and, ok), x, 0.0) if ok else x
+
+        values = []
+        for q in range(4):
+            value = None
+            for dy in range(3):
+                near = tap(q, 3 * dy + 1)
+                if q > 0:
+                    near = near + tap(q - 1, 3 * dy)
+                if q < 3:
+                    near = near + tap(q + 1, 3 * dy + 2)
+                term = moved(near, dy, 1)
+                if q == 0:
+                    term = term + moved(tap(3, 3 * dy), dy, 0)
+                if q == 3:
+                    term = term + moved(tap(0, 3 * dy + 2), dy, 2)
+                value = term if value is None else value + term
+            values.append(value * blend[q, :, at : at + lanes])
+        return values
+
+    def pack_side(x, rim):
+        dense = pltpu.roll(x[0], (half - rim) % half, 1)
+        for q in range(1, 4):
+            turned = pltpu.roll(x[q], (HALO * q - rim) % half, 1)
+            dense = jnp.where(where_b // HALO == q, turned, dense)
+        return dense
+
+    def pack_pair(x, pair, h):
+        even, odds = x[2 * pair], x[2 * pair + 1]
+        if h == 0:
+            odds = pltpu.roll(odds, half // 2, 1)
+        else:
+            even = pltpu.roll(even, half // 2, 1)
+        return jnp.where(lower_half, even, odds)
+
+    def send_rims(wanted):
+        for k, (dr, dc) in FAR_FIRST:
+            if wanted(dr):
+
+                @pl.when(exists(dr, dc))
+                def _():
+                    copies(k, dr, dc)[1].start()
+
+    middle = side_cells // 2
+    upper = colours(0, middle)
+    up_rows = [v[0:4] for v in blended(upper, 0)]
+    for k, rim in ((0, 0), (1, side_cells - HALO)):
+        up_out[k] = pack_side(up_rows, rim)
+    for pair in range(2):
+        vert_out[0, pair] = pack_pair(up_rows, pair, 0)
+    send_rims(lambda dr: dr < 0)
+    for_all(lambda n, m: batch(cells, n, send1, recv1).wait_send())
+
+    lower = colours(middle, side_cells)
+    both = [jnp.concatenate([a, b], axis=1) for a, b in zip(upper, lower)]
+    values = blended(both, 0)
     for h in range(2):
+        here = [v[0:4, h * half : (h + 1) * half] for v in values]
+        for q in range(4):
+            own[h, q] = here[q]
         for k, rim in ((0, 0), (1, side_cells - HALO)):
-            dense = pltpu.roll(own[h, 0], (half - rim) % half, 1)
-            for q in range(1, 4):
-                turned = pltpu.roll(own[h, q], (HALO * q - rim) % half, 1)
-                dense = jnp.where(where_b // HALO == q, turned, dense)
-            side_out[k, h] = dense
-        for pair in range(2):
-            even, odds = own[h, 2 * pair], own[h, 2 * pair + 1]
-            if h == 0:
-                odds = pltpu.roll(odds, half // 2, 1)
-            else:
-                even = pltpu.roll(even, half // 2, 1)
-            vert_out[h, pair] = jnp.where(lower_half, even, odds)
-
-    for k, (dr, dc) in FAR_FIRST:
-
-        @pl.when(exists(dr, dc))
-        def _():
-            copies(k, dr, dc)[1].start()
+            side_out[k, h] = pack_side(here, rim)
+        if h == 1:
+            for pair in range(2):
+                vert_out[h, pair] = pack_pair(here, pair, h)
+    send_rims(lambda dr: dr >= 0)
 
     lane_row = iota((8, half), 1) // side_cells
     sublane = iota((8, half), 0)
@@ -555,7 +598,6 @@
             blocks.append(jnp.concatenate([spread_rows(p, c, keep[h]) for p in mine], axis=1))
     mine = placed(blocks, places[0])
 
-    for_all(lambda n, m: batch(cells, n, send1, recv1).wait_send())
     for_all(lambda n, m: batch(rims, m, send2, recv2).wait_recv())
 
     blocks = []
@@ -616,6 +658,7 @@
                 pltpu.VMEM((2, 4 * half, inner), BF16),
                 pltpu.VMEM((2, 4, 4, half), F32),
                 pltpu.VMEM((2, 4, 4, half), F32),
+                pltpu.VMEM((2, 4, half), F32),
                 pltpu.VMEM((2, 2, 4, half), F32),
                 pltpu.VMEM((2, 2, 4, half), F32),
                 pltpu.VMEM((12, 4, half), F32),

time: 12 us -> 11.9 us (level)
  no operation moved by 1% of the time
where the time goes in v10:
time: 11.9 us; the launch traced here: 11.7 us
  Pallas kernels  11.1 us (93%)
  local copies, waits for them, and re-layouts  0.61 us (5%)
    pallas_call x1, Pallas kernels, per_device(): pl.pallas_call(functools.partial(kernel, nr, nc), out_shape=pltpu.VMEM((w...  11.1 us
    unnamed x1, local copies, waits for them, and re-layouts  0.61 us

profile of v10, /device:TPU:1, one launch (start us, length us, event | category | flops | bytes accessed | tf_op | source)
XLA Modules:
  0.0 11.7 jit_solution(5398667541347582673)
XLA Ops:
  0.0 11.1 %decode.1 = f32[3,16,16]{2,1,0:T(8,128)S(1)} custom-call(bf16[4,4,4]{2,1,0:T(4,128)(2,1)} %refs_0_.1, bf16[9,4,512]{2,1,0:T(4,128)(2,1)} %refs_1_.1, bf16[9,256,512]{2,1,0:T(8,128)(2,1)} %refs_2_.1, bf16[9,128,256]{2,1,0:T(8,128)(2,1)} %refs_3_.1, bf16[9,3,128]{2,1,0:T(4,128)(2,1)} %refs_4_.1, s32[4,32]{1,0:T(4,128)} %refs_5_.1, s32[4,32]{1,0:T(4,128)} %refs_6_.1, ...), custom_call_target="tpu_custom_call" | custom-call | tf_op jit(solution)/shard_map/decode/pallas_call | solution.py:638
  11.1 0.6 %copy.11 = f32[3,16,16]{2,1,0:T(8,128)} copy(f32[3,16,16]{2,1,0:T(8,128)S(1)} %decode.1) | data formatting | bytes 6144

commit v11 on v10

--- a/solution.py
+++ b/solution.py
@@ -144,7 +144,7 @@
 
 def body(
     nr, nc, lat, w_in, w_mid, w_low, w_out, ramp_r, ramp_c, lim_r, lim_c, out,
-    cells, wi, wm, wl, wo, tables, limits, wi32, wo32, wc, wmt, wlt,
+    cells, lined, wi, wm, wl, wo, tables, limits, wi32, wo32, wc, wmt, wlt,
     blend, inverse, places, scales, own, up_out, side_out, vert_out, rims,
     ready, recv1, recv2, local_sem,
 ):
@@ -428,18 +428,20 @@
         for n, side in enumerate(sides):
             scales[h, n] = side
 
+    lined[...] = jnp.zeros(lined.shape, F32)
     for_all(lambda n, m: batch(cells, n, send1, recv1).wait_recv())
 
-    cell = [cells[k].astype(F32) for k in range(9)]
     pieces = [[], [], []]
+    cuts = (slice(tile - HALO, tile), slice(0, tile), slice(0, HALO))
     for c in range(chans):
-        for j, cut in enumerate((slice(tile - HALO, tile), slice(0, tile), slice(0, HALO))):
-            upper, middle, lower = (cell[3 * i + j][c][:, cut] for i in range(3))
-            zero = jnp.zeros((1, middle.shape[1]), F32)
-            upper, lower = upper[tile - HALO :], lower[:HALO]
-            pieces[0].append(jnp.concatenate([zero, upper, middle, lower[:-1]], axis=0))
-            pieces[1].append(jnp.concatenate([upper, middle, lower], axis=0))
-            pieces[2].append(jnp.concatenate([upper[1:], middle, lower, zero], axis=0))
+        for j, cut in enumerate(cuts):
+            at = 1
+            for i in range(3):
+                block = cells[3 * i + j, c].astype(F32)[cuts[i], :]
+                lined[c, j, at : at + block.shape[0], 0:tile] = block
+                at += block.shape[0]
+            for dy in range(3):
+                pieces[dy].append(lined[c, j, dy : dy + side_cells, cut])
     pieces = pieces[0] + pieces[1] + pieces[2]
     tall = jnp.concatenate(pieces + [jnp.zeros((side_cells, 128 - 3 * wide), F32)], axis=1)
     shape = (side_cells, side_cells, 128)
@@ -613,7 +615,8 @@
             blocks.append(
                 jnp.concatenate([spread_rows(p, c, m) for p, m in zip(got, masks)], axis=1)
             )
-    out[...] = (mine + placed(blocks, places[1])).reshape(3, inner, inner)
+    rest = dot(jnp.concatenate(blocks, axis=0).astype(BF16), places[1])
+    out[...] = (mine + rest).reshape(3, inner, inner)
 
     for_all(lambda n, m: batch(rims, m, send2, recv2).wait_send())
 
@@ -642,6 +645,7 @@
             out_specs=pl.BlockSpec(memory_space=pltpu.VMEM),
             scratch_shapes=[
                 pltpu.VMEM((max(9, 6 + 2 * (lat.shape[1] // HALO)),) + lat.shape, BF16),
+                pltpu.VMEM((lat.shape[0], 3, 16, 128), F32),
                 pltpu.VMEM(w_in.shape, BF16),
                 pltpu.VMEM(w_mid.shape, BF16),
                 pltpu.VMEM(w_low.shape, BF16),

time: 11.9 us -> 11.8 us (level)
  no operation moved by 1% of the time
where the time goes in v11:
time: 11.8 us; the launch traced here: 11.7 us
  Pallas kernels  11.1 us (94%)
  local copies, waits for them, and re-layouts  0.61 us (5%)
    pallas_call x1, Pallas kernels, per_device(): pl.pallas_call(functools.partial(kernel, nr, nc), out_shape=pltpu.VMEM((w...  11.1 us
    unnamed x1, local copies, waits for them, and re-layouts  0.61 us

profile of v11, /device:TPU:1, one launch (start us, length us, event | category | flops | bytes accessed | tf_op | source)
XLA Modules:
  0.0 11.7 jit_solution(12289097016067885683)
XLA Ops:
  0.0 11.1 %decode.1 = f32[3,16,16]{2,1,0:T(8,128)S(1)} custom-call(bf16[4,4,4]{2,1,0:T(4,128)(2,1)} %refs_0_.1, bf16[9,4,512]{2,1,0:T(4,128)(2,1)} %refs_1_.1, bf16[9,256,512]{2,1,0:T(8,128)(2,1)} %refs_2_.1, bf16[9,128,256]{2,1,0:T(8,128)(2,1)} %refs_3_.1, bf16[9,3,128]{2,1,0:T(4,128)(2,1)} %refs_4_.1, s32[4,32]{1,0:T(4,128)} %refs_5_.1, s32[4,32]{1,0:T(4,128)} %refs_6_.1, ...), custom_call_target="tpu_custom_call" | custom-call | tf_op jit(solution)/shard_map/decode/pallas_call | solution.py:641
  11.1 0.6 %copy.11 = f32[3,16,16]{2,1,0:T(8,128)} copy(f32[3,16,16]{2,1,0:T(8,128)S(1)} %decode.1) | data formatting | bytes 6144

commit v12 on v11

--- a/solution.py
+++ b/solution.py
@@ -145,7 +145,7 @@
 def body(
     nr, nc, lat, w_in, w_mid, w_low, w_out, ramp_r, ramp_c, lim_r, lim_c, out,
     cells, lined, wi, wm, wl, wo, tables, limits, wi32, wo32, wc, wmt, wlt,
-    blend, inverse, places, scales, own, up_out, side_out, vert_out, rims,
+    blend, inverse, places, blend_up, scales, own, side_out, vert_out, rims,
     ready, recv1, recv2, local_sem,
 ):
     row, col = lax.axis_index("rows"), lax.axis_index("cols")
@@ -229,16 +229,11 @@
         if dr == 0:
             return rims.at[pl.ds(2 * left_right, 2)]
         if dc == 0:
-            return rims.at[pl.ds(8 + 2 * up_down, 2)]
-        return rims.at[4 + 2 * left_right + up_down]
+            return rims.at[pl.ds(12 + 2 * up_down, 2)]
+        return rims.at[pl.ds(4 + 4 * left_right + 2 * up_down, 2)]
 
     def packed(dr, dc):
-        up_down, left_right = (dr + 1) // 2, (dc + 1) // 2
-        if dr == 0:
-            return side_out.at[left_right]
-        if dc == 0:
-            return vert_out.at[up_down]
-        return up_out.at[left_right] if dr < 0 else side_out.at[left_right, 1]
+        return side_out.at[(dc + 1) // 2] if dr == 0 else vert_out.at[(dr + 1) // 2]
 
     def rows_of(slot, dr):
         if dr == 0:
@@ -275,7 +270,7 @@
 
                 @pl.when(jnp.logical_and(above_below == v, beside == h))
                 def _():
-                    wait(v + v * h + lat.shape[1] // HALO * h, 2 * (v + h) + v * h)
+                    wait(v + v * h + lat.shape[1] // HALO * h, 2 * (v + h + v * h))
 
     def batch(ref, n, send, recv):
         part = ref.at[pl.ds(0, n), :, pl.ds(0, HALO)] if ref is cells else ref.at[pl.ds(0, n)]
@@ -295,7 +290,7 @@
             slot = cells.at[(1 + dr) * 3 + 1 + dc]
             slot[...] = jnp.zeros(slot.shape, BF16)
             pixels = slot_of(dr, dc)
-            pixels[...] = jnp.zeros(pixels.shape, F32)
+            pixels[...] = jnp.zeros(pixels.shape, BF16)
 
     @pl.when(earlier > 0)
     def _():
@@ -374,6 +369,8 @@
     for q in range(4):
         cw = col_w[:, q * span : (q + 1) * span]
         blend[q] = jnp.broadcast_to(row_w[0:1] * cw[0:1], (8, span))
+        upper = jnp.broadcast_to((row_w[0:1] * cw[0:1])[:, :half], (8, half))
+        blend_up[q] = pltpu.roll(upper, half // 2, 1) if q % 2 else upper
         inverse[q] = jnp.broadcast_to(
             1.0 / jnp.where(inside, row_w[1:2] * cw[1:2], 1.0), (8, span)
         )
@@ -404,7 +401,8 @@
     from_left = place_dst == 4 * (slot % HALO) + slot // HALO
     from_right = place_dst == 4 * (tile - HALO + slot % HALO) + slot // HALO
     pair_q = 2 * (place_src // half - 2) + place_src % half // (half // 2)
-    from_pair = place_dst == 4 * (slot - HALO) + pair_q
+    beside_by = jnp.where(slot < HALO, tile, jnp.where(slot < HALO + tile, 0, -tile))
+    from_pair = place_dst == 4 * (slot - HALO + beside_by) + pair_q
     part = place_src // half
     places[1] = jnp.where(
         part == 0, from_left.astype(F32), jnp.where(part == 1, from_right.astype(F32), from_pair.astype(F32))
@@ -424,7 +422,12 @@
                 even = pltpu.roll(even, half // 2, 1)
             else:
                 odds = pltpu.roll(odds, half // 2, 1)
-            sides.append(jnp.where(lower_half, even, odds))
+            inner_scale = jnp.where(lower_half, even, odds)
+            onward = pltpu.roll(inner_scale, half - tile, 1)
+            back = pltpu.roll(inner_scale, tile, 1)
+            outer_scale = jnp.where(where_b < HALO, onward, back)
+            within = jnp.logical_and(where_b >= HALO, where_b < HALO + tile)
+            sides.append(jnp.where(within, inner_scale, outer_scale))
         for n, side in enumerate(sides):
             scales[h, n] = side
 
@@ -497,38 +500,37 @@
             got += [both[:, :half], both[:, half:]]
         return got
 
-    def blended(colour, at):
+    def blended(colour, weight, turn):
         lanes = colour[0].shape[1]
-        sub_b = iota((8, lanes), 1) % side_cells
-        sub_r = iota((8, lanes), 1) // side_cells
-        row_ok = [sub_r > 0, None, sub_r < lanes // side_cells - 1]
-        col_ok = [sub_b > 0, None, sub_b < side_cells - 1]
-
         def tap(q, t):
             return colour[q][8 * t : 8 * t + 8]
 
-        def moved(x, dy, dx):
-            shift = (side_cells * (1 - dy) + 1 - dx) % lanes
+        def moved(x, dy, dx, by):
+            at = (iota((8, lanes), 1) + lanes - by) % lanes
+            sub_b, sub_r = at % side_cells, at // side_cells
+            row_ok = [sub_r > 0, None, sub_r < lanes // side_cells - 1]
+            col_ok = [sub_b > 0, None, sub_b < side_cells - 1]
+            shift = (side_cells * (1 - dy) + 1 - dx + by) % lanes
             x = pltpu.roll(x, shift, 1) if shift else x
             ok = [m for m in (row_ok[dy], col_ok[dx]) if m is not None]
             return jnp.where(functools.reduce(jnp.logical_and, ok), x, 0.0) if ok else x
 
         values = []
         for q in range(4):
-            value = None
+            value, by = None, turn * (q % 2)
             for dy in range(3):
                 near = tap(q, 3 * dy + 1)
                 if q > 0:
                     near = near + tap(q - 1, 3 * dy)
                 if q < 3:
                     near = near + tap(q + 1, 3 * dy + 2)
-                term = moved(near, dy, 1)
+                term = moved(near, dy, 1, by)
                 if q == 0:
-                    term = term + moved(tap(3, 3 * dy), dy, 0)
+                    term = term + moved(tap(3, 3 * dy), dy, 0, by)
                 if q == 3:
-                    term = term + moved(tap(0, 3 * dy + 2), dy, 2)
+                    term = term + moved(tap(0, 3 * dy + 2), dy, 2, by)
                 value = term if value is None else value + term
-            values.append(value * blend[q, :, at : at + lanes])
+            values.append(value * weight[q])
         return values
 
     def pack_side(x, rim):
@@ -538,13 +540,9 @@
             dense = jnp.where(where_b // HALO == q, turned, dense)
         return dense
 
-    def pack_pair(x, pair, h):
-        even, odds = x[2 * pair], x[2 * pair + 1]
-        if h == 0:
-            odds = pltpu.roll(odds, half // 2, 1)
-        else:
-            even = pltpu.roll(even, half // 2, 1)
-        return jnp.where(lower_half, even, odds)
+    def pack_pair(x, pair):
+        even = pltpu.roll(x[2 * pair], half // 2, 1)
+        return jnp.where(lower_half, even, x[2 * pair + 1])
 
     def send_rims(wanted):
         for k, (dr, dc) in FAR_FIRST:
@@ -556,26 +554,24 @@
 
     middle = side_cells // 2
     upper = colours(0, middle)
-    up_rows = [v[0:4] for v in blended(upper, 0)]
-    for k, rim in ((0, 0), (1, side_cells - HALO)):
-        up_out[k] = pack_side(up_rows, rim)
+    up_rows = [v[0:4] for v in blended(upper, blend_up, half // 2)]
     for pair in range(2):
-        vert_out[0, pair] = pack_pair(up_rows, pair, 0)
+        both = jnp.where(lower_half, up_rows[2 * pair], up_rows[2 * pair + 1])
+        vert_out[0, pair] = both.astype(BF16)
     send_rims(lambda dr: dr < 0)
     for_all(lambda n, m: batch(cells, n, send1, recv1).wait_send())
 
     lower = colours(middle, side_cells)
     both = [jnp.concatenate([a, b], axis=1) for a, b in zip(upper, lower)]
-    values = blended(both, 0)
+    values = blended(both, blend, 0)
     for h in range(2):
         here = [v[0:4, h * half : (h + 1) * half] for v in values]
         for q in range(4):
             own[h, q] = here[q]
         for k, rim in ((0, 0), (1, side_cells - HALO)):
-            side_out[k, h] = pack_side(here, rim)
-        if h == 1:
-            for pair in range(2):
-                vert_out[h, pair] = pack_pair(here, pair, h)
+            side_out[k, h] = pack_side(here, rim).astype(BF16)
+    for pair in range(2):
+        vert_out[1, pair] = pack_pair(here, pair).astype(BF16)
     send_rims(lambda dr: dr >= 0)
 
     lane_row = iota((8, half), 1) // side_cells
@@ -606,11 +602,14 @@
     for c in range(3):
         for h in range(2):
             got = [
-                (rims[h] + rims[4 + h]) * scales[h, 0],
-                (rims[2 + h] + rims[6 + h]) * scales[h, 1],
-                rims[8 + 2 * h] * scales[h, 2],
-                rims[9 + 2 * h] * scales[h, 3],
+                rims[h].astype(F32) * scales[h, 0],
+                rims[2 + h].astype(F32) * scales[h, 1],
             ]
+            for pair in range(2):
+                left, right, straight = (rims[at + 2 * h + pair].astype(F32) for at in (4, 8, 12))
+                straight = jnp.where(where_b < HALO, right, straight)
+                straight = jnp.where(where_b < HALO + tile, straight, left)
+                got.append(straight * scales[h, 2 + pair])
             masks = [keep[h], keep[h], beyond_row[h], beyond_row[h]]
             blocks.append(
                 jnp.concatenate([spread_rows(p, c, m) for p, m in zip(got, masks)], axis=1)
@@ -660,12 +659,12 @@
                 pltpu.VMEM((4, 8, 2 * half), F32),
                 pltpu.VMEM((4, 8, 2 * half), F32),
                 pltpu.VMEM((2, 4 * half, inner), BF16),
+                pltpu.VMEM((4, 8, half), F32),
                 pltpu.VMEM((2, 4, 4, half), F32),
                 pltpu.VMEM((2, 4, 4, half), F32),
-                pltpu.VMEM((2, 4, half), F32),
-                pltpu.VMEM((2, 2, 4, half), F32),
-                pltpu.VMEM((2, 2, 4, half), F32),
-                pltpu.VMEM((12, 4, half), F32),
+                pltpu.VMEM((2, 2, 4, half), BF16),
+                pltpu.VMEM((2, 2, 4, half), BF16),
+                pltpu.VMEM((16, 4, half), BF16),
                 pltpu.SemaphoreType.REGULAR((5,)),
                 dma,
                 dma,

time: 11.8 us -> 11.8 us (level)
  no operation moved by 1% of the time
where the time goes in v12:
time: 11.8 us; the launch traced here: 11.6 us
  Pallas kernels  11 us (93%)
  local copies, waits for them, and re-layouts  0.61 us (5%)
    pallas_call x1, Pallas kernels, per_device(): pl.pallas_call(functools.partial(kernel, nr, nc), out_shape=pltpu.VMEM((w...  11 us
    unnamed x1, local copies, waits for them, and re-layouts  0.61 us

profile of v12, /device:TPU:1, one launch (start us, length us, event | category | flops | bytes accessed | tf_op | source)
XLA Modules:
  0.0 11.6 jit_solution(14380732933474888699)
XLA Ops:
  0.0 11.0 %decode.1 = f32[3,16,16]{2,1,0:T(8,128)S(1)} custom-call(bf16[4,4,4]{2,1,0:T(4,128)(2,1)} %refs_0_.1, bf16[9,4,512]{2,1,0:T(4,128)(2,1)} %refs_1_.1, bf16[9,256,512]{2,1,0:T(8,128)(2,1)} %refs_2_.1, bf16[9,128,256]{2,1,0:T(8,128)(2,1)} %refs_3_.1, bf16[9,3,128]{2,1,0:T(4,128)(2,1)} %refs_4_.1, s32[4,32]{1,0:T(4,128)} %refs_5_.1, s32[4,32]{1,0:T(4,128)} %refs_6_.1, ...), custom_call_target="tpu_custom_call" | custom-call | tf_op jit(solution)/shard_map/decode/pallas_call | solution.py:640
  11.0 0.6 %copy.11 = f32[3,16,16]{2,1,0:T(8,128)} copy(f32[3,16,16]{2,1,0:T(8,128)S(1)} %decode.1) | data formatting | bytes 6144

commit v13 on v12

--- a/solution.py
+++ b/solution.py
@@ -296,6 +296,17 @@
     def _():
         pl.semaphore_wait(barrier, earlier)
 
+    hurry = jnp.logical_or(greeted_by(1, -1), greeted_by(1, 1))
+
+    @pl.when(hurry)
+    def _():
+        loads[0].wait()
+        for k, dc in ((7, 1), (5, -1)):
+
+            @pl.when(greeted_by(1, dc))
+            def _():
+                copies(k, 1, dc)[0].start()
+
     for k, (dr, dc) in FAR_FIRST:
         if dr <= 0:
             by = greeted_by(dr, dc)
@@ -306,12 +317,14 @@
                     ready.at[READY[7 - k]], inc=1, device_id=device(dr, dc), device_id_type=MESH
                 )
 
-    loads[0].wait()
+    @pl.when(jnp.logical_not(hurry))
+    def _():
+        loads[0].wait()
+
     for k, (dr, dc) in FAR_FIRST:
-        by = greeted_by(dr, dc)
-        if by is not None:
-
-            @pl.when(by)
+        if dr <= 0:
+
+            @pl.when(greeted_by(dr, dc))
             def _():
                 copies(k, dr, dc)[0].start()
 
@@ -325,7 +338,6 @@
                 copies(k, dr, dc)[0].start()
 
     below = [e for e in enumerate(AROUND) if e[1][0] > 0]
-    hurry = jnp.logical_or(greeted_by(1, -1), greeted_by(1, 1))
     send_later(below, hurry)
     send_later([e for e in enumerate(AROUND) if e[1][0] == 0])
 

time: 11.8 us -> 11.8 us (level)
  no operation moved by 1% of the time
where the time goes in v13:
time: 11.8 us; the launch traced here: 11.6 us
  Pallas kernels  11 us (93%)
  local copies, waits for them, and re-layouts  0.61 us (5%)
    pallas_call x1, Pallas kernels, per_device(): pl.pallas_call(functools.partial(kernel, nr, nc), out_shape=pltpu.VMEM((w...  11 us
    unnamed x1, local copies, waits for them, and re-layouts  0.61 us

profile of v13, /device:TPU:1, one launch (start us, length us, event | category | flops | bytes accessed | tf_op | source)
XLA Modules:
  0.0 11.6 jit_solution(16527352739100183532)
XLA Ops:
  0.0 11.0 %decode.1 = f32[3,16,16]{2,1,0:T(8,128)S(1)} custom-call(bf16[4,4,4]{2,1,0:T(4,128)(2,1)} %refs_0_.1, bf16[9,4,512]{2,1,0:T(4,128)(2,1)} %refs_1_.1, bf16[9,256,512]{2,1,0:T(8,128)(2,1)} %refs_2_.1, bf16[9,128,256]{2,1,0:T(8,128)(2,1)} %refs_3_.1, bf16[9,3,128]{2,1,0:T(4,128)(2,1)} %refs_4_.1, s32[4,32]{1,0:T(4,128)} %refs_5_.1, s32[4,32]{1,0:T(4,128)} %refs_6_.1, ...), custom_call_target="tpu_custom_call" | custom-call | tf_op jit(solution)/shard_map/decode/pallas_call | solution.py:652
  11.0 0.6 %copy.11 = f32[3,16,16]{2,1,0:T(8,128)} copy(f32[3,16,16]{2,1,0:T(8,128)S(1)} %decode.1) | data formatting | bytes 6144

commit v14 on v13

--- a/solution.py
+++ b/solution.py
@@ -15,7 +15,7 @@
 AROUND = [(dr, dc) for dr in (-1, 0, 1) for dc in (-1, 0, 1) if (dr, dc) != (0, 0)]
 FAR_FIRST = sorted(enumerate(AROUND), key=lambda e: -abs(e[1][0]) - abs(e[1][1]))
 BY_COLUMN = [3 * (t % 3) + t // 3 for t in range(9)]
-READY = {k: n for n, k in enumerate((3, 4, 5, 6, 7))}
+READY = {3: 0, 4: 0, 5: 1, 6: 2, 7: 3}
 
 
 def iota(shape, dim):
@@ -339,7 +339,17 @@
 
     below = [e for e in enumerate(AROUND) if e[1][0] > 0]
     send_later(below, hurry)
-    send_later([e for e in enumerate(AROUND) if e[1][0] == 0])
+
+    @pl.when(jnp.logical_and(odd, beside > 0))
+    def _():
+        pl.semaphore_wait(ready.at[READY[3]], beside)
+
+    for k, dc in ((3, -1), (4, 1)):
+
+        @pl.when(leads(0, dc))
+        def _():
+            copies(k, 0, dc)[0].start()
+
 
     tile = lat.shape[1]
     side_cells = tile + 2 * HALO
@@ -677,7 +687,7 @@
                 pltpu.VMEM((2, 2, 4, half), BF16),
                 pltpu.VMEM((2, 2, 4, half), BF16),
                 pltpu.VMEM((16, 4, half), BF16),
-                pltpu.SemaphoreType.REGULAR((5,)),
+                pltpu.SemaphoreType.REGULAR((4,)),
                 dma,
                 dma,
             ],

time: 11.8 us -> 11.8 us (level)
  no operation moved by 1% of the time
where the time goes in v14:
time: 11.8 us; the launch traced here: 11.6 us
  Pallas kernels  11 us (93%)
  local copies, waits for them, and re-layouts  0.61 us (5%)
    pallas_call x1, Pallas kernels, per_device(): pl.pallas_call(functools.partial(kernel, nr, nc), out_shape=pltpu.VMEM((w...  11 us
    unnamed x1, local copies, waits for them, and re-layouts  0.61 us

profile of v14, /device:TPU:1, one launch (start us, length us, event | category | flops | bytes accessed | tf_op | source)
XLA Modules:
  0.0 11.6 jit_solution(7171982744763708822)
XLA Ops:
  0.0 11.0 %decode.1 = f32[3,16,16]{2,1,0:T(8,128)S(1)} custom-call(bf16[4,4,4]{2,1,0:T(4,128)(2,1)} %refs_0_.1, bf16[9,4,512]{2,1,0:T(4,128)(2,1)} %refs_1_.1, bf16[9,256,512]{2,1,0:T(8,128)(2,1)} %refs_2_.1, bf16[9,128,256]{2,1,0:T(8,128)(2,1)} %refs_3_.1, bf16[9,3,128]{2,1,0:T(4,128)(2,1)} %refs_4_.1, s32[4,32]{1,0:T(4,128)} %refs_5_.1, s32[4,32]{1,0:T(4,128)} %refs_6_.1, ...), custom_call_target="tpu_custom_call" | custom-call | tf_op jit(solution)/shard_map/decode/pallas_call | solution.py:662
  11.0 0.6 %copy.11 = f32[3,16,16]{2,1,0:T(8,128)} copy(f32[3,16,16]{2,1,0:T(8,128)S(1)} %decode.1) | data formatting | bytes 6144
